TPU v7x, 8 devices: a whole 2x2x1 slice. The times are simulated.
8 devices in a mesh: dp: 2 (over z, y), sp: 4 (over x, core).
Axes of the slice: x: 2, y: 2, z: 1, core: 2. Of those that a mesh axis runs over, the one named last changes fastest.
Arguments:
- latents: bfloat16 [32, 8, 64, 1280], P('dp', 'sp'), parts along dimension 0
- time_emb: bfloat16 [32, 1280], P('dp'), parts along dimension 0
- context: bfloat16 [32, 77, 2048], P('dp'), parts along dimension 0
- res_norm: float32 [2, 2, 2, 1280], replicated
- res_conv_w: bfloat16 [2, 2, 3, 3, 1280, 1280], replicated
- res_conv_b: float32 [2, 2, 1280], replicated
- res_temb_w: bfloat16 [2, 1280, 1280], replicated
- res_temb_b: float32 [2, 1280], replicated
- tr_norm: float32 [2, 1280], replicated
- proj_w: bfloat16 [2, 1280, 1280], replicated
- proj_b: float32 [2, 1280], replicated
- ln_par: float32 [2, 3, 2, 1280], replicated
- self_qkv: bfloat16 [2, 3, 1280, 20, 64], replicated
- cross_q: bfloat16 [2, 1280, 20, 64], replicated
- cross_kv: bfloat16 [2, 2, 2048, 20, 64], replicated
- attn_out: bfloat16 [2, 2, 20, 64, 1280], replicated
- attn_b: float32 [2, 2, 1280], replicated
- ff_in_w: bfloat16 [2, 1280, 10240], replicated
- ff_in_b: float32 [2, 10240], replicated
- ff_out_w: bfloat16 [2, 5120, 1280], replicated
- ff_out_b: float32 [2, 1280], replicated
Outputs:
- output: bfloat16 [32, 8, 64, 1280], P('dp', 'sp'), parts along dimension 0
There are 2 independent parts. A program takes and returns all parts, laid end to end along the dimension named above; an argument that names none is the same for every part.
All inputs are finite; a program needn't handle non-finite values.
Results may differ from a plain program's by a relative error of at most 0.0196347.
Values are sent between devices in bfloat16 or wider.
A program may use at most 1.25 GiB of HBM per device.

v0:
```python
import functools
import math
import jax
import jax.numpy as jnp
from jax import lax
from jax.sharding import PartitionSpec as P

NUM_GROUPS = 32


def group_norm_sp(values, norm_gain, norm_bias, eps_val, sp_size):
    batch_n, rows_n, cols_n, chan_n = values.shape
    grouped = values.astype(jnp.float32).reshape(batch_n, rows_n, cols_n, NUM_GROUPS, chan_n // NUM_GROUPS)
    local_sums = jnp.stack([grouped.sum(axis=(1, 2, 4)), (grouped * grouped).sum(axis=(1, 2, 4))])
    total_sums = lax.psum(local_sums, 'sp')
    count_n = rows_n * sp_size * cols_n * (chan_n // NUM_GROUPS)
    grp_mean = total_sums[0] / count_n
    grp_var = total_sums[1] / count_n - grp_mean * grp_mean
    inv_std = lax.rsqrt(grp_var + eps_val)
    normed = (grouped - grp_mean[:, None, None, :, None]) * inv_std[:, None, None, :, None]
    return normed.reshape(batch_n, rows_n, cols_n, chan_n) * norm_gain + norm_bias


def conv_rows(act_in, kernel, sp_size):
    to_next = [(position, position + 1) for position in range(sp_size - 1)]
    to_prev = [(position + 1, position) for position in range(sp_size - 1)]
    from_above = lax.ppermute(act_in[:, -1:], 'sp', to_next)
    from_below = lax.ppermute(act_in[:, :1], 'sp', to_prev)
    padded = jnp.concatenate([from_above, act_in, from_below], axis=1)
    return lax.conv_general_dilated(padded, kernel, (1, 1), ((0, 0), (1, 1)), dimension_numbers=('NHWC', 'HWIO', 'NHWC'), preferred_element_type=jnp.float32)


def resnet_local(latents, time_emb, res_index, res_norm, res_conv_w, res_conv_b, res_temb_w, res_temb_b, sp_size):
    first_act = jax.nn.silu(group_norm_sp(latents, res_norm[res_index, 0, 0], res_norm[res_index, 0, 1], 1e-5, sp_size)).astype(jnp.bfloat16)
    time_proj = jnp.dot(jax.nn.silu(time_emb.astype(jnp.float32)).astype(jnp.bfloat16), res_temb_w[res_index], preferred_element_type=jnp.float32) + res_temb_b[res_index]
    hidden = (conv_rows(first_act, res_conv_w[res_index, 0], sp_size) + res_conv_b[res_index, 0] + time_proj[:, None, None, :]).astype(jnp.bfloat16)
    second_act = jax.nn.silu(group_norm_sp(hidden, res_norm[res_index, 1, 0], res_norm[res_index, 1, 1], 1e-5, sp_size)).astype(jnp.bfloat16)
    update = conv_rows(second_act, res_conv_w[res_index, 1], sp_size) + res_conv_b[res_index, 1]
    return (latents.astype(jnp.float32) + update).astype(jnp.bfloat16)


def layer_norm(values, norm_gain, norm_bias):
    centered = values.astype(jnp.float32)
    centered = centered - centered.mean(axis=-1, keepdims=True)
    variance = (centered * centered).mean(axis=-1, keepdims=True)
    return (centered * lax.rsqrt(variance + 1e-5) * norm_gain + norm_bias).astype(jnp.bfloat16)


def attend_block(q_blk, k_all, v_all):
    scale_f = 1.0 / math.sqrt(q_blk.shape[-1])
    scores = jnp.einsum('bqhd,bkhd->bhqk', q_blk, k_all, preferred_element_type=jnp.float32) * scale_f
    row_exp = jnp.exp(scores - scores.max(axis=-1, keepdims=True))
    row_sum = row_exp.sum(axis=-1)
    row_out = jnp.einsum('bhqk,bkhd->bqhd', row_exp.astype(jnp.bfloat16), v_all, preferred_element_type=jnp.float32)
    return (row_out / jnp.swapaxes(row_sum, 1, 2)[..., None]).astype(jnp.bfloat16)


def attend_rows(q_all, k_all, v_all, rows_n):
    batch_n, tok_n, head_n, dim_n = q_all.shape
    q_rows = jnp.swapaxes(q_all.reshape(batch_n, rows_n, tok_n // rows_n, head_n, dim_n), 0, 1)
    attended = lax.map(lambda q_row: attend_block(q_row, k_all, v_all), q_rows)
    return jnp.swapaxes(attended, 0, 1).reshape(batch_n, tok_n, head_n, dim_n)


def transformer_local(hidden, context, tr_norm, proj_w, proj_b, ln_par, self_qkv, cross_q, cross_kv, attn_out, attn_b, ff_in_w, ff_in_b, ff_out_w, ff_out_b, sp_size):
    batch_n, rows_n, cols_n, chan_n = hidden.shape
    normed = group_norm_sp(hidden, tr_norm[0], tr_norm[1], 1e-6, sp_size).astype(jnp.bfloat16).reshape(batch_n, rows_n * cols_n, chan_n)
    hidden_tok = (jnp.einsum('bnc,cd->bnd', normed, proj_w[0], preferred_element_type=jnp.float32) + proj_b[0]).astype(jnp.bfloat16)
    ff_width = ff_out_w.shape[1]
    for layer_i in range(ln_par.shape[0]):
        normed = layer_norm(hidden_tok, ln_par[layer_i, 0, 0], ln_par[layer_i, 0, 1])
        qkv_loc = jnp.einsum('bnc,jchd->jbnhd', normed, self_qkv[layer_i], preferred_element_type=jnp.float32).astype(jnp.bfloat16)
        qkv_heads = lax.all_to_all(qkv_loc, 'sp', 3, 2, tiled=True)
        attended = attend_rows(qkv_heads[0], qkv_heads[1], qkv_heads[2], rows_n * sp_size)
        att_rows = lax.all_to_all(attended, 'sp', 1, 2, tiled=True)
        hidden_tok = (hidden_tok.astype(jnp.float32) + jnp.einsum('bnhd,hdc->bnc', att_rows, attn_out[layer_i, 0], preferred_element_type=jnp.float32) + attn_b[layer_i, 0]).astype(jnp.bfloat16)
        normed = layer_norm(hidden_tok, ln_par[layer_i, 1, 0], ln_par[layer_i, 1, 1])
        q_cross = jnp.einsum('bnc,chd->bnhd', normed, cross_q[layer_i], preferred_element_type=jnp.float32).astype(jnp.bfloat16)
        kv_cross = jnp.einsum('btc,jchd->jbthd', context, cross_kv[layer_i], preferred_element_type=jnp.float32).astype(jnp.bfloat16)
        crossed = attend_block(q_cross, kv_cross[0], kv_cross[1])
        hidden_tok = (hidden_tok.astype(jnp.float32) + jnp.einsum('bnhd,hdc->bnc', crossed, attn_out[layer_i, 1], preferred_element_type=jnp.float32) + attn_b[layer_i, 1]).astype(jnp.bfloat16)
        normed = layer_norm(hidden_tok, ln_par[layer_i, 2, 0], ln_par[layer_i, 2, 1])
        ff_proj = jnp.einsum('bnc,cf->bnf', normed, ff_in_w[layer_i], preferred_element_type=jnp.float32) + ff_in_b[layer_i]
        gated_act = (ff_proj[..., :ff_width] * jax.nn.gelu(ff_proj[..., ff_width:], approximate=False)).astype(jnp.bfloat16)
        hidden_tok = (hidden_tok.astype(jnp.float32) + jnp.einsum('bnf,fc->bnc', gated_act, ff_out_w[layer_i], preferred_element_type=jnp.float32) + ff_out_b[layer_i]).astype(jnp.bfloat16)
    out_tok = jnp.einsum('bnc,cd->bnd', hidden_tok, proj_w[1], preferred_element_type=jnp.float32) + proj_b[1] + hidden.reshape(batch_n, rows_n * cols_n, chan_n).astype(jnp.float32)
    return out_tok.astype(jnp.bfloat16).reshape(batch_n, rows_n, cols_n, chan_n)


def device_block(latents, time_emb, context, res_norm, res_conv_w, res_conv_b, res_temb_w, res_temb_b, tr_norm, proj_w, proj_b, ln_par, self_qkv, cross_q, cross_kv, attn_out, attn_b, ff_in_w, ff_in_b, ff_out_w, ff_out_b, sp_size):
    first_out = resnet_local(latents, time_emb, 0, res_norm, res_conv_w, res_conv_b, res_temb_w, res_temb_b, sp_size)
    middle = transformer_local(first_out, context, tr_norm, proj_w, proj_b, ln_par, self_qkv, cross_q, cross_kv, attn_out, attn_b, ff_in_w, ff_in_b, ff_out_w, ff_out_b, sp_size)
    return resnet_local(middle, time_emb, 1, res_norm, res_conv_w, res_conv_b, res_temb_w, res_temb_b, sp_size)


def solution(mesh):
    sp_size = mesh.shape['sp']
    row_spec = P('dp', 'sp')
    part_spec = P('dp')
    in_specs = (row_spec, part_spec, part_spec) + (P(),) * 18
    body_fn = functools.partial(device_block, sp_size=sp_size)
    return jax.shard_map(body_fn, mesh=mesh, in_specs=in_specs, out_specs=row_spec, check_vma=False)
```

profile of v0, /device:TPU:0, one launch (start us, length us, event | category | flops | bytes accessed | tf_op | source)
XLA Modules:
  0.0 2089.1 jit_solution(4383112875334805855)
XLA Ops:
  38.6 73.5 %convert_reduce_fusion.8 = (f32[16,1280]{1,0:T(8,128)S(1)}, f32[16,1280]{1,0:T(8,128)S(1)}, bf16[16,2,64,1280]{3,0,2,1:T(8,128)(2,1)}) fusion(f32[16,1280]{1,0:T(8,128)S(1)} %fusion.349, f32[1280]{0:T(1024)S(1)} %get-tuple-element.133, bf16[2,2,3,3,1280,1280]{5,4,3,2,1,0:T(8,128)(2,1)} %param.29, bf16[16,1,64,1280]{3,0,2,1:T(8,128)(2,1)} %copy-done.42, ...), kind=kOutput, calls=%fused_computation.123 | convolution fusion | flops 59818598400 | bytes 45470720 | tf_op jit(solution)/shard_map/conv_general_dilated | solution.py:30
  112.8 36.6 %psum.36 = f32[2,16,32]{2,1,0:T(8,128)S(1)} all-reduce(f32[2,16,32]{2,1,0:T(8,128)S(1)} %pad_maximum_fusion.1), channel_id=1, replica_groups=mesh['dp'=2,'sp'=4] {'sp'}, use_global_device_ids=true, to_apply=%region_9.10 | all-reduce | flops 1024 | bytes 8192 | tf_op jit(solution)/shard_map/psum | solution.py:15
  169.9 86.8 %convert_reduce_fusion.9 = (f32[16,1280]{1,0:T(8,128)S(1)}, f32[16,1280]{1,0:T(8,128)S(1)}, bf16[16,2,64,1280]{3,0,2,1:T(8,128)(2,1)}) fusion(f32[1280]{0:T(1024)S(1)} %get-tuple-element.132, bf16[2,2,3,3,1280,1280]{5,4,3,2,1,0:T(8,128)(2,1)} %param.29, bf16[16,1,64,1280]{3,0,2,1:T(8,128)(2,1)} %copy-done.41, bf16[16,2,64,1280]{3,0,2,1:T(8,128)(2,1)} %copy-done.2, ...), kind=kOutput, calls=%fused_computation.261 | convolution fusion | flops 59821219840 | bytes 50631680 | tf_op jit(solution)/shard_map/conv_general_dilated | solution.py:30
  257.3 36.6 %psum.37 = f32[2,16,32]{2,1,0:T(8,128)S(1)} all-reduce(f32[2,16,32]{2,1,0:T(8,128)S(1)} %pad_maximum_fusion.2), channel_id=1, replica_groups=mesh['dp'=2,'sp'=4] {'sp'}, use_global_device_ids=true, to_apply=%region_14.15 | all-reduce | flops 1024 | bytes 8192 | tf_op jit(solution)/shard_map/psum | solution.py:15
  312.1 25.1 %convert_bitcast_fusion.1 = bf16[3,16,128,20,64]{2,4,3,0,1:T(8,128)(2,1)S(1)} fusion(bf16[2,3,1280,20,64]{2,4,3,1,0:T(8,128)(2,1)} %param.37, bf16[16,128,1280]{2,1,0:T(8,128)(2,1)S(1)} %get-tuple-element.194, f32[1280]{0:T(1024)S(1)} %copy-done.31, f32[1280]{0:T(1024)S(1)} %copy-done.32, f32[16,128]{1,0:T(8,128)S(1)} %add_rsqrt_fusion.5, ...), kind=kOutput, calls=%fused_computation.117 | convolution fusion | flops 20156252160 | bytes 30828544 | tf_op jit(solution)/shard_map/bnc,jchd->jbnhd/dot_general | solution.py:72
  351.5 171.5 %all-to-all-done = bf16[3,16,128,20,64]{2,4,0,1,3:T(8,128)(2,1)} async-done(((bf16[3,16,128,20,64]{2,4,0,1,3:T(8,128)(2,1)}), bf16[3,16,128,20,64]{2,4,0,1,3:T(8,128)(2,1)}, u32[]{:S(2)}, u32[]{:S(2)}) %all-to-all-start) | async-done | bytes 15728672 | tf_op jit(solution)/shard_map/all_to_all | solution.py:73
  522.9 18.0 copy.193
  604.2 90.2 %while.20 = (s32[]{:T(128)}, bf16[8,16,64,5,64]{4,2,3,1,0:T(8,128)(2,1)}, bf16[8,16,64,5,64]{4,2,3,1,0:T(8,128)(2,1)}, bf16[16,512,5,64]{1,3,2,0:T(8,128)(2,1)}, bf16[16,512,5,64]{1,3,2,0:T(8,128)(2,1)}, /*index=5*/s32[]{:T(128)}) while((s32[]{:T(128)}, bf16[8,16,64,5,64]{4,2,3,1,0:T(8,128)(2,1)}, bf16[8,16,64,5,64]{4,2,3,1,0:T(8,128)(2,1)}, ...), condition=%wide.region_20.21_spmd, body=%wide.region_17.20_spmd.sunk | while | flops 692705280 | bytes 60396660 | solution.py:61
  725.6 40.4 %convert_bitcast_fusion.3 = bf16[2,16,77,20,64]{2,4,1,3,0:T(8,128)(2,1)} fusion(bf16[2,2,2048,20,64]{2,4,3,1,0:T(8,128)(2,1)} %param.39, bf16[16,77,2048,1,1]{2,0,1,4,3:T(8,128)(2,1)} %bitcast.478), kind=kOutput, calls=%fused_computation.251 | convolution fusion | flops 12921610240 | bytes 21839872 | tf_op jit(solution)/shard_map/btc,jchd->jbthd/dot_general | solution.py:79
  852.1 17.4 convert_reduce_fusion.5
  878.0 64.3 %broadcast_add_fusion.1 = f32[16,128,10240]{2,1,0:T(8,128)} fusion(f32[10240]{0:T(1024)S(1)} %bitcast.465, bf16[2,1280,10240]{2,1,0:T(8,128)(2,1)} %param.42, bf16[16,128,1280]{2,1,0:T(8,128)(2,1)S(1)} %fusion.544), kind=kOutput, calls=%fused_computation.69 | convolution fusion | flops 53708062720 | bytes 115384320 | tf_op jit(solution)/shard_map/bnc,cf->bnf/dot_general | solution.py:83
  942.3 126.6 %convert_reduce_fusion.4 = (f32[16,128]{1,0:T(8,128)S(1)}, bf16[16,128,1280]{2,1,0:T(8,128)(2,1)S(1)}) fusion(f32[1280]{0:T(1024)S(1)} %copy-done.38, bf16[2,5120,1280]{2,1,0:T(8,128)(2,1)} %param.44, f32[16,128,10240]{2,1,0:T(8,128)} %broadcast_add_fusion.1, bf16[16,128,1280]{2,1,0:T(8,128)(2,1)S(1)} %bitcast.444), kind=kOutput, calls=%fused_computation.110 | convolution fusion | flops 27551332352 | bytes 107492352 | tf_op jit(solution)/shard_map/bnf,fc->bnc/dot_general | solution.py:85
  1070.5 24.7 %convert_bitcast_fusion = bf16[3,16,128,20,64]{2,4,3,0,1:T(8,128)(2,1)S(1)} fusion(bf16[2,3,1280,20,64]{2,4,3,1,0:T(8,128)(2,1)} %param.37, bf16[16,128,1280]{2,1,0:T(8,128)(2,1)S(1)} %get-tuple-element.202, f32[1280]{0:T(1024)S(1)} %copy-done.27, f32[1280]{0:T(1024)S(1)} %copy-done.28, f32[16,128]{1,0:T(8,128)S(1)} %add_rsqrt_fusion.2, ...), kind=kOutput, calls=%fused_computation.107 | convolution fusion | flops 20156252160 | bytes 30828544 | tf_op jit(solution)/shard_map/bnc,jchd->jbnhd/dot_general | solution.py:72
  1097.3 175.9 %all_to_all.66 = bf16[3,16,128,20,64]{2,4,0,1,3:T(8,128)(2,1)} all-to-all(bf16[3,16,128,20,64]{2,4,0,1,3:T(8,128)(2,1)S(1)} %copy.114), channel_id=1, replica_groups=mesh['dp'=2,'sp'=4] {'sp'}, dimensions={3} | all-to-all | bytes 31457280 | tf_op jit(solution)/shard_map/all_to_all | solution.py:73
  1273.3 18.0 copy.192
  1354.4 90.2 %while.21 = (s32[]{:T(128)}, bf16[8,16,64,5,64]{4,2,3,1,0:T(8,128)(2,1)}, bf16[8,16,64,5,64]{4,2,3,1,0:T(8,128)(2,1)}, bf16[16,512,5,64]{1,3,2,0:T(8,128)(2,1)}, bf16[16,512,5,64]{1,3,2,0:T(8,128)(2,1)}, /*index=5*/s32[]{:T(128)}) while((s32[]{:T(128)}, bf16[8,16,64,5,64]{4,2,3,1,0:T(8,128)(2,1)}, bf16[8,16,64,5,64]{4,2,3,1,0:T(8,128)(2,1)}, ...), condition=%wide.region_32.33_spmd, body=%wide.region_29.32_spmd.sunk | while | flops 692705280 | bytes 60396660 | solution.py:61
  1476.0 40.4 %convert_bitcast_fusion.2 = bf16[2,16,77,20,64]{2,4,1,3,0:T(8,128)(2,1)} fusion(bf16[2,2,2048,20,64]{2,4,3,1,0:T(8,128)(2,1)} %param.39, bf16[16,77,2048,1,1]{2,0,1,4,3:T(8,128)(2,1)} %bitcast.479), kind=kOutput, calls=%fused_computation.249 | convolution fusion | flops 12921610240 | bytes 21839872 | tf_op jit(solution)/shard_map/btc,jchd->jbthd/dot_general | solution.py:79
  1604.1 17.4 convert_reduce_fusion.2
  1630.2 64.3 %broadcast_add_fusion = f32[16,128,10240]{2,1,0:T(8,128)} fusion(f32[10240]{0:T(1024)S(1)} %bitcast.464, bf16[2,1280,10240]{2,1,0:T(8,128)(2,1)} %param.42, bf16[16,128,1280]{2,1,0:T(8,128)(2,1)S(1)} %fusion.542), kind=kOutput, calls=%fused_computation.55 | convolution fusion | flops 53708062720 | bytes 115384320 | tf_op jit(solution)/shard_map/bnc,cf->bnf/dot_general | solution.py:83
  1694.5 128.5 %fusion.147.clone.3.clone.5 = bf16[16,128,1280]{2,1,0:T(8,128)(2,1)} fusion(bf16[16,128,1280]{2,1,0:T(8,128)(2,1)S(1)} %bitcast.446, bf16[2,5120,1280]{2,1,0:T(8,128)(2,1)} %param.44, f32[16,128,10240]{2,1,0:T(8,128)} %broadcast_add_fusion, f32[1280]{0:T(1024)S(1)} %copy-done.37), kind=kOutput, calls=%fused_computation.193.clone.clone.clone.clone.clone.clone.clone.2 | convolution fusion | flops 27546091520 | bytes 107484160 | tf_op jit(solution)/shard_map/bnf,fc->bnc/dot_general | solution.py:85
  1823.0 16.7 fusion.484
  1877.9 73.6 %convert_reduce_fusion.1 = (f32[16,1280]{1,0:T(8,128)S(1)}, f32[16,1280]{1,0:T(8,128)S(1)}, bf16[16,2,64,1280]{3,0,2,1:T(8,128)(2,1)}) fusion(f32[16,1280]{1,0:T(8,128)S(1)} %fusion.352, f32[1280]{0:T(1024)S(1)} %copy-done.35, bf16[2,2,3,3,1280,1280]{5,4,3,2,1,0:T(8,128)(2,1)} %param.29, bf16[16,1,64,1280]{3,0,2,1:T(8,128)(2,1)S(1)} %collective-permute-done.5, ...), kind=kOutput, calls=%fused_computation.100 | convolution fusion | flops 59818598400 | bytes 45470720 | tf_op jit(solution)/shard_map/conv_general_dilated | solution.py:30
  1952.1 36.6 %psum.39 = f32[2,16,32]{2,1,0:T(8,128)S(1)} all-reduce(f32[2,16,32]{2,1,0:T(8,128)S(1)} %pad_maximum_fusion.4), channel_id=1, replica_groups=mesh['dp'=2,'sp'=4] {'sp'}, use_global_device_ids=true, to_apply=%region_48.49 | all-reduce | flops 1024 | bytes 8192 | tf_op jit(solution)/shard_map/psum | solution.py:15
  2006.7 75.5 %add_convert_fusion = bf16[16,2,64,1280]{3,0,2,1:T(8,128)(2,1)} fusion(f32[16,2,64,1280]{3,0,2,1:T(8,128)} %bitcast.434, bf16[2,2,3,3,1280,1280]{5,4,3,2,1,0:T(8,128)(2,1)} %param.29, bf16[16,1,64,1280]{3,0,2,1:T(8,128)(2,1)} %copy-done.44, bf16[16,2,64,1280]{3,0,2,1:T(8,128)(2,1)S(1)} %fusion.157, bf16[16,1,64,1280]{3,0,2,1:T(8,128)(2,1)} %copy-done.43, ...), kind=kOutput, calls=%fused_computation.245 | convolution fusion | flops 59808153600 | bytes 55710720 | tf_op jit(solution)/shard_map/conv_general_dilated | solution.py:30
  (406 shorter events, 717.8 us)
Async XLA Ops:
  28.4 5.8 collective-permute-start
  29.8 7.3 collective-permute-start.1
  158.4 5.9 collective-permute-start.2
  159.9 8.4 collective-permute-start.3
  344.6 178.3 %all-to-all-start = ((bf16[3,16,128,20,64]{2,4,0,1,3:T(8,128)(2,1)}), bf16[3,16,128,20,64]{2,4,0,1,3:T(8,128)(2,1)}, u32[]{:S(2)}, u32[]{:S(2)}) async-start(bf16[3,16,128,20,64]{2,4,0,1,3:T(8,128)(2,1)} %copy.104), calls=%async_computation | async-start | bytes 31457280 | tf_op jit(solution)/shard_map/all_to_all | solution.py:73
  720.3 64.4 %all-to-all-start.1 = ((bf16[4,2,327680]{2,1,0:T(2,128)(2,1)}), bf16[4,2,327680]{2,1,0:T(2,128)(2,1)}, u32[]{:S(2)}, u32[]{:S(2)}) async-start(bf16[4,2,327680]{2,1,0:T(2,128)(2,1)} %reshape.337), calls=%async_computation.1 | async-start | bytes 10485760 | tf_op jit(solution)/shard_map/all_to_all | solution.py:75
  725.6 40.4 %copy-start.20 = (f32[2,2,1280]{2,1,0:T(2,128)S(1)}, f32[2,2,1280]{2,1,0:T(2,128)}, u32[]{:S(2)}) copy-start(f32[2,2,1280]{2,1,0:T(2,128)} %param.41) | copy-start | bytes 61444
  873.6 68.7 %slice-start.2 = ((s8[5242880]{0:T(1024)(128)(4,1)}), s8[4194304]{0:T(1024)(128)(4,1)S(1)}, s32[]{:S(2)}) async-start(s8[5242880]{0:T(1024)(128)(4,1)} %bitcast.443), calls=%async_computation.6 | async-start | bytes 8388608
  877.9 64.3 %slice-start.3 = ((s8[5242880]{0:T(1024)(128)(4,1)}), s8[1048576]{0:T(1024)(128)(4,1)S(1)}, s32[]{:S(2)}) async-start(s8[5242880]{0:T(1024)(128)(4,1)} %bitcast.443), calls=%async_computation.7 | async-start | bytes 2097152
  877.9 64.3 %copy-start.38 = (f32[1280]{0:T(1024)S(1)}, f32[1280]{0:T(1024)}, u32[]{:S(2)}) copy-start(f32[1280]{0:T(1024)} %get-tuple-element.211) | copy-start | bytes 15364
  942.2 128.3 %copy-start.27 = (f32[1280]{0:T(1024)S(1)}, f32[1280]{0:T(1024)}, u32[]{:S(2)}) copy-start(f32[1280]{0:T(1024)} %get-tuple-element.114) | copy-start | bytes 15364
  942.2 128.3 %copy-start.28 = (f32[1280]{0:T(1024)S(1)}, f32[1280]{0:T(1024)}, u32[]{:S(2)}) copy-start(f32[1280]{0:T(1024)} %get-tuple-element.115) | copy-start | bytes 15364
  1470.6 66.3 %all-to-all-start.3 = ((bf16[4,2,327680]{2,1,0:T(2,128)(2,1)}), bf16[4,2,327680]{2,1,0:T(2,128)(2,1)}, u32[]{:S(2)}, u32[]{:S(2)}) async-start(bf16[4,2,327680]{2,1,0:T(2,128)(2,1)} %reshape.339), calls=%async_computation.3 | async-start | bytes 10485760 | tf_op jit(solution)/shard_map/all_to_all | solution.py:75
  1625.6 68.9 %slice-start.4 = ((s8[5242880]{0:T(1024)(128)(4,1)}), s8[4194304]{0:T(1024)(128)(4,1)S(1)}, s32[]{:S(2)}) async-start(s8[5242880]{0:T(1024)(128)(4,1)} %bitcast.445), calls=%async_computation.8 | async-start | bytes 8388608
  1630.2 64.3 %slice-start.5 = ((s8[5242880]{0:T(1024)(128)(4,1)}), s8[1048576]{0:T(1024)(128)(4,1)S(1)}, s32[]{:S(2)}) async-start(s8[5242880]{0:T(1024)(128)(4,1)} %bitcast.445), calls=%async_computation.9 | async-start | bytes 2097152
  1630.2 64.3 %copy-start.37 = (f32[1280]{0:T(1024)S(1)}, f32[1280]{0:T(1024)}, u32[]{:S(2)}) copy-start(f32[1280]{0:T(1024)} %get-tuple-element.212) | copy-start | bytes 15364
  1694.5 128.5 %copy-start.3 = (f32[16,128,1280]{2,0,1:T(8,128)S(1)}, f32[16,128,1280]{2,0,1:T(8,128)}, u32[]{:S(2)}) copy-start(f32[16,128,1280]{2,0,1:T(8,128)} %bitcast_convert_fusion) | copy-start | bytes 31457284
  1694.5 128.5 %copy-start.36 = (f32[1280]{0:T(1024)S(1)}, f32[1280]{0:T(1024)}, u32[]{:S(2)}) copy-start(f32[1280]{0:T(1024)} %get-tuple-element.143) | copy-start | bytes 15364
  1869.1 5.8 collective-permute-start.4
  1870.6 7.3 collective-permute-start.5
  1877.9 111.5 %copy-start.17 = (f32[1280]{0:T(1024)S(1)}, f32[1280]{0:T(1024)}, u32[]{:S(2)}) copy-start(f32[1280]{0:T(1024)} %get-tuple-element.123) | copy-start | bytes 15364
  1877.9 111.5 %copy-start.18 = (f32[1280]{0:T(1024)S(1)}, f32[1280]{0:T(1024)}, u32[]{:S(2)}) copy-start(f32[1280]{0:T(1024)} %get-tuple-element.130) | copy-start | bytes 15364
  1995.2 5.9 collective-permute-start.6
  1996.7 8.4 collective-permute-start.7
  (78 other events, 584.1 us)
where the time goes:
time: 2130 us; the launch traced here: 2090 us
  matrix products  1080 us (51%)
  local copies, waits for them, and re-layouts  347 us (16%)
  blocking collectives  311 us (15%)
  waiting for transfers between devices  197 us (9%)
  other arithmetic  122 us (6%)
  starting transfers between devices  28.7 us (1%)
    conv_general_dilated x4, matrix products, conv_rows(): lax.conv_general_dilated(padded, kernel, (1, 1), ((0, 0), (1, 1)), dimens...  309 us
    dot_general x2, matrix products, transformer_local(): jnp.einsum('bnf,fc->bnc', gated_act, ff_out_w[layer_i], preferred_element...  255 us
    all_to_all x1, blocking collectives, transformer_local(): qkv_heads = lax.all_to_all(qkv_loc, 'sp', 3, 2, tiled=True)  176 us
    all_to_all x1, waiting for transfers between devices, transformer_local(): qkv_heads = lax.all_to_all(qkv_loc, 'sp', 3, 2, tiled=True)  171 us
    psum x5, blocking collectives, group_norm_sp(): total_sums = lax.psum(local_sums, 'sp')  135 us
    dot_general x2, matrix products, transformer_local(): jnp.einsum('bnc,cf->bnf', normed, ff_in_w[layer_i], preferred_element_typ...  129 us
    dot_general x18, matrix products, attend_block(): jnp.einsum('bqhd,bkhd->bhqk', q_blk, k_all, preferred_element_type=jnp.fl...  105 us
    dot_general x2, matrix products, transformer_local(): jnp.einsum('btc,jchd->jbthd', context, cross_kv[layer_i], preferred_eleme...  80.7 us
  transfers between devices with their start and end apart: 11, of which 10 were waited for; matrix products, arithmetic and copies ran while one was open for 6% of the time, Pallas kernels for 0%

commit v1 on v0

v1 whole, which is shorter than its diff:
```python
import functools
import math
import jax
import jax.numpy as jnp
from jax import lax
from jax.sharding import PartitionSpec as P

NUM_GROUPS = 32


def group_norm(values, norm_gain, norm_bias, eps_val):
    batch_n, rows_n, cols_n, chan_n = values.shape
    grouped = values.astype(jnp.float32).reshape(batch_n, rows_n, cols_n, NUM_GROUPS, chan_n // NUM_GROUPS)
    count_n = rows_n * cols_n * (chan_n // NUM_GROUPS)
    grp_mean = grouped.sum(axis=(1, 2, 4)) / count_n
    grp_var = (grouped * grouped).sum(axis=(1, 2, 4)) / count_n - grp_mean * grp_mean
    inv_std = lax.rsqrt(grp_var + eps_val)
    normed = (grouped - grp_mean[:, None, None, :, None]) * inv_std[:, None, None, :, None]
    return normed.reshape(batch_n, rows_n, cols_n, chan_n) * norm_gain + norm_bias


def conv_rows(act_in, kernel):
    return lax.conv_general_dilated(act_in, kernel, (1, 1), ((1, 1), (1, 1)), dimension_numbers=('NHWC', 'HWIO', 'NHWC'), preferred_element_type=jnp.float32)


def resnet_local(latents, time_emb, res_index, res_norm, res_conv_w, res_conv_b, res_temb_w, res_temb_b):
    first_act = jax.nn.silu(group_norm(latents, res_norm[res_index, 0, 0], res_norm[res_index, 0, 1], 1e-5)).astype(jnp.bfloat16)
    time_proj = jnp.dot(jax.nn.silu(time_emb.astype(jnp.float32)).astype(jnp.bfloat16), res_temb_w[res_index], preferred_element_type=jnp.float32) + res_temb_b[res_index]
    hidden = (conv_rows(first_act, res_conv_w[res_index, 0]) + res_conv_b[res_index, 0] + time_proj[:, None, None, :]).astype(jnp.bfloat16)
    second_act = jax.nn.silu(group_norm(hidden, res_norm[res_index, 1, 0], res_norm[res_index, 1, 1], 1e-5)).astype(jnp.bfloat16)
    update = conv_rows(second_act, res_conv_w[res_index, 1]) + res_conv_b[res_index, 1]
    return (latents.astype(jnp.float32) + update).astype(jnp.bfloat16)


def layer_norm(values, norm_gain, norm_bias):
    centered = values.astype(jnp.float32)
    centered = centered - centered.mean(axis=-1, keepdims=True)
    variance = (centered * centered).mean(axis=-1, keepdims=True)
    return (centered * lax.rsqrt(variance + 1e-5) * norm_gain + norm_bias).astype(jnp.bfloat16)


def attend_block(q_blk, k_all, v_all):
    scale_f = 1.0 / math.sqrt(q_blk.shape[-1])
    scores = jnp.einsum('bqhd,bkhd->bhqk', q_blk, k_all, preferred_element_type=jnp.float32) * scale_f
    row_exp = jnp.exp(scores - scores.max(axis=-1, keepdims=True))
    row_sum = row_exp.sum(axis=-1)
    row_out = jnp.einsum('bhqk,bkhd->bqhd', row_exp.astype(jnp.bfloat16), v_all, preferred_element_type=jnp.float32)
    return (row_out / jnp.swapaxes(row_sum, 1, 2)[..., None]).astype(jnp.bfloat16)


def transformer_local(hidden, context, tr_norm, proj_w, proj_b, ln_par, self_qkv, cross_q, cross_kv, attn_out, attn_b, ff_in_w, ff_in_b, ff_out_w, ff_out_b):
    batch_n, rows_n, cols_n, chan_n = hidden.shape
    normed = group_norm(hidden, tr_norm[0], tr_norm[1], 1e-6).astype(jnp.bfloat16).reshape(batch_n, rows_n * cols_n, chan_n)
    hidden_tok = (jnp.einsum('bnc,cd->bnd', normed, proj_w[0], preferred_element_type=jnp.float32) + proj_b[0]).astype(jnp.bfloat16)
    ff_width = ff_out_w.shape[1]
    for layer_i in range(ln_par.shape[0]):
        normed = layer_norm(hidden_tok, ln_par[layer_i, 0, 0], ln_par[layer_i, 0, 1])
        qkv_loc = jnp.einsum('bnc,jchd->jbnhd', normed, self_qkv[layer_i], preferred_element_type=jnp.float32).astype(jnp.bfloat16)
        attended = attend_block(qkv_loc[0], qkv_loc[1], qkv_loc[2])
        hidden_tok = (hidden_tok.astype(jnp.float32) + jnp.einsum('bnhd,hdc->bnc', attended, attn_out[layer_i, 0], preferred_element_type=jnp.float32) + attn_b[layer_i, 0]).astype(jnp.bfloat16)
        normed = layer_norm(hidden_tok, ln_par[layer_i, 1, 0], ln_par[layer_i, 1, 1])
        q_cross = jnp.einsum('bnc,chd->bnhd', normed, cross_q[layer_i], preferred_element_type=jnp.float32).astype(jnp.bfloat16)
        kv_cross = jnp.einsum('btc,jchd->jbthd', context, cross_kv[layer_i], preferred_element_type=jnp.float32).astype(jnp.bfloat16)
        crossed = attend_block(q_cross, kv_cross[0], kv_cross[1])
        hidden_tok = (hidden_tok.astype(jnp.float32) + jnp.einsum('bnhd,hdc->bnc', crossed, attn_out[layer_i, 1], preferred_element_type=jnp.float32) + attn_b[layer_i, 1]).astype(jnp.bfloat16)
        normed = layer_norm(hidden_tok, ln_par[layer_i, 2, 0], ln_par[layer_i, 2, 1])
        ff_proj = jnp.einsum('bnc,cf->bnf', normed, ff_in_w[layer_i], preferred_element_type=jnp.float32) + ff_in_b[layer_i]
        gated_act = (ff_proj[..., :ff_width] * jax.nn.gelu(ff_proj[..., ff_width:], approximate=False)).astype(jnp.bfloat16)
        hidden_tok = (hidden_tok.astype(jnp.float32) + jnp.einsum('bnf,fc->bnc', gated_act, ff_out_w[layer_i], preferred_element_type=jnp.float32) + ff_out_b[layer_i]).astype(jnp.bfloat16)
    out_tok = jnp.einsum('bnc,cd->bnd', hidden_tok, proj_w[1], preferred_element_type=jnp.float32) + proj_b[1] + hidden.reshape(batch_n, rows_n * cols_n, chan_n).astype(jnp.float32)
    return out_tok.astype(jnp.bfloat16).reshape(batch_n, rows_n, cols_n, chan_n)


def device_block(latents, time_emb, context, res_norm, res_conv_w, res_conv_b, res_temb_w, res_temb_b, tr_norm, proj_w, proj_b, ln_par, self_qkv, cross_q, cross_kv, attn_out, attn_b, ff_in_w, ff_in_b, ff_out_w, ff_out_b, sp_size):
    own_n = latents.shape[0] // sp_size
    first = lax.axis_index('sp') * own_n
    whole = lax.all_to_all(latents, 'sp', 0, 1, tiled=True)
    time_own = lax.dynamic_slice_in_dim(time_emb, first, own_n, 0)
    ctx_own = lax.dynamic_slice_in_dim(context, first, own_n, 0)
    first_out = resnet_local(whole, time_own, 0, res_norm, res_conv_w, res_conv_b, res_temb_w, res_temb_b)
    middle = transformer_local(first_out, ctx_own, tr_norm, proj_w, proj_b, ln_par, self_qkv, cross_q, cross_kv, attn_out, attn_b, ff_in_w, ff_in_b, ff_out_w, ff_out_b)
    last = resnet_local(middle, time_own, 1, res_norm, res_conv_w, res_conv_b, res_temb_w, res_temb_b)
    return lax.all_to_all(last, 'sp', 1, 0, tiled=True)


def solution(mesh):
    sp_size = mesh.shape['sp']
    row_spec = P('dp', 'sp')
    part_spec = P('dp')
    in_specs = (row_spec, part_spec, part_spec) + (P(),) * 18
    body_fn = functools.partial(device_block, sp_size=sp_size)
    return jax.shard_map(body_fn, mesh=mesh, in_specs=in_specs, out_specs=row_spec, check_vma=False)
```

time: 2130 us -> 1600 us (0.75); the launches traced: 2090 us -> 1590 us
  blocking collectives: 311 us -> 62 us
  local copies, waits for them, and re-layouts: 347 us -> 147 us
  waiting for transfers between devices: 197 us -> 28.7 us
  matrix products: 1080 us -> 1160 us
  other arithmetic: 122 us -> 188 us
  starting transfers between devices: 28.7 us -> 5.18 us
    all_to_all x3 -> x1, waiting for transfers between devices: 176 us -> 28.7 us  [device_block(): whole = lax.all_to_all(latents, 'sp', 0, 1, tiled=True)]
    psum x5 -> x0, blocking collectives: 135 us -> none  [group_norm_sp(): total_sums = lax.psum(local_sums, 'sp')]
    conv_general_dilated x4, matrix products: 309 us -> 438 us  [conv_rows(): lax.conv_general_dilated(act_in, kernel, (1, 1), ((1, 1), (1, 1)), dimens...]
    all_to_all x1, blocking collectives: 176 us -> 62 us  [device_block(): return lax.all_to_all(last, 'sp', 1, 0, tiled=True)]
    all_to_all x6 -> x1, local copies, waits for them, and re-layouts: 70 us -> 2.7 us  [device_block(): return lax.all_to_all(last, 'sp', 1, 0, tiled=True)]
    dot_general x2, matrix products: 80.7 us -> 17.8 us  [transformer_local(): jnp.einsum('btc,jchd->jbthd', context, cross_kv[layer_i], preferred_eleme...]
    squeeze x6 -> x0, local copies, waits for them, and re-layouts: 59.8 us -> none  [the longest x2 25.1 us: transformer_local(): crossed = attend_block(q_cross, kv_cross[0], kv_cross[1])]
    unnamed x122 -> x128, local copies, waits for them, and re-layouts: 58.1 us -> 11.4 us
  transfers between devices with their start and end apart: 11 -> 1, of which waited for: 10 -> 1; matrix products, arithmetic and copies ran while one was open for 6% -> 2% of each run, Pallas kernels for 0% -> 0%
where the time goes in v1:
time: 1600 us; the launch traced here: 1590 us
  matrix products  1160 us (72%)
  other arithmetic  188 us (12%)
  local copies, waits for them, and re-layouts  147 us (9%)
  blocking collectives  62 us (4%)
  waiting for transfers between devices  28.7 us (2%)
    conv_general_dilated x4, matrix products, conv_rows(): lax.conv_general_dilated(act_in, kernel, (1, 1), ((1, 1), (1, 1)), dimens...  438 us
    dot_general x2, matrix products, transformer_local(): jnp.einsum('bnf,fc->bnc', gated_act, ff_out_w[layer_i], preferred_element...  258 us
    dot_general x2, matrix products, transformer_local(): jnp.einsum('bnc,cf->bnf', normed, ff_in_w[layer_i], preferred_element_typ...  140 us
    dot_general x4, matrix products, attend_block(): jnp.einsum('bqhd,bkhd->bhqk', q_blk, k_all, preferred_element_type=jnp.fl...  96.2 us
    reduce_sum x4, other arithmetic, attend_block(): row_sum = row_exp.sum(axis=-1)  69.1 us
    dot_general x2, matrix products, attend_block(): jnp.einsum('bhqk,bkhd->bqhd', row_exp.astype(jnp.bfloat16), v_all, prefer...  66.3 us
    all_to_all x1, blocking collectives, device_block(): return lax.all_to_all(last, 'sp', 1, 0, tiled=True)  62 us
    dot_general x2, matrix products, transformer_local(): jnp.einsum('bnc,jchd->jbnhd', normed, self_qkv[layer_i], preferred_elemen...  53.3 us
  transfers between devices with their start and end apart: 1, of which 1 were waited for; matrix products, arithmetic and copies ran while one was open for 2% of the time, Pallas kernels for 0%

profile of v1, /device:TPU:0, one launch (start us, length us, event | category | flops | bytes accessed | tf_op | source)
XLA Modules:
  0.0 1587.3 jit_solution(16175539492483660381)
XLA Ops:
  36.7 28.7 %all-to-all-done = bf16[16,2,64,1280]{3,2,1,0:T(8,128)(2,1)} async-done(((bf16[16,2,64,1280]{3,2,1,0:T(8,128)(2,1)}), bf16[16,2,64,1280]{3,2,1,0:T(8,128)(2,1)}, u32[]{:S(2)}, u32[]{:S(2)}) %all-to-all-start) | async-done | bytes 5242912 | tf_op jit(solution)/shard_map/all_to_all | solution.py:77
  116.4 134.6 %convert_multiply_fusion.1 = (f32[8,32,9,1280]{3,1,2,0:T(8,128)}, bf16[8,32,9,1280]{3,1,2,0:T(8,128)(2,1)S(1)}) fusion(f32[8,32,9,1280]{3,0,2,1:T(8,128)} %bitcast.435, f32[1280]{0:T(1024)S(1)} %get-tuple-element.33, bf16[2,2,3,3,1280,1280]{5,4,3,2,1,0:T(8,128)(2,1)} %param.25, bf16[8,4,8,11,1280]{4,0,3,2,1:T(8,128)(2,1)} %fusion.145, ...), kind=kOutput, calls=%fused_computation.249 | convolution fusion | flops 62303109120 | bytes 66196768 | tf_op jit(solution)/shard_map/conv_general_dilated | solution.py:23
  257.7 15.5 copy.99
  296.3 84.4 %fusion.151 = f32[8,32,9,1280]{3,1,2,0:T(8,128)} fusion(bf16[2,2,3,3,1280,1280]{5,4,3,2,1,0:T(8,128)(2,1)} %param.25, f32[1280]{0:T(1024)S(1)} %copy-done.51, bf16[8,32,11,1280]{3,1,2,0:T(8,128)(2,1)S(1)} %fusion.465), kind=kOutput, calls=%fused_computation.221 | convolution fusion | flops 62288363520 | bytes 48501760 | tf_op jit(solution)/shard_map/conv_general_dilated | solution.py:23
  380.7 15.6 copy.101
  430.4 26.5 %convert_bitcast_fusion.1 = bf16[3,4,512,20,64]{2,4,3,0,1:T(8,128)(2,1)} fusion(bf16[2,3,1280,20,64]{2,4,3,1,0:T(8,128)(2,1)} %param.33, bf16[4,512,1280]{2,1,0:T(8,128)(2,1)S(1)} %get-tuple-element.67, f32[1280]{0:T(1024)S(1)} %copy-done.39, f32[1280]{0:T(1024)S(1)} %copy-done.40, f32[4,512]{1,0:T(4,128)S(1)} %add_rsqrt_fusion.5, ...), kind=kOutput, calls=%fused_computation.90 | convolution fusion | flops 20156252160 | bytes 30828544 | tf_op jit(solution)/shard_map/bnc,jchd->jbnhd/dot_general | solution.py:58
  456.9 33.0 %multiply_reduce_fusion.1 = (f32[4,20,512]{2,1,0:T(8,128)S(1)}, f32[4,20,512,512]{2,3,1,0:T(8,128)}) fusion(bf16[3,4,512,20,64]{2,4,3,0,1:T(8,128)(2,1)} %convert_bitcast_fusion.1), kind=kOutput, calls=%fused_computation.3 | convolution fusion | flops 2726256640 | bytes 94535680 | tf_op jit(solution)/shard_map/bqhd,bkhd->bhqk/dot_general | solution.py:44
  489.9 26.1 %fusion = f32[4,20,512]{2,1,0:T(8,128)S(1)} fusion(f32[4,20,512,512]{2,3,1,0:T(8,128)} %get-tuple-element.69, f32[4,20,512]{2,1,0:T(8,128)S(1)} %get-tuple-element.68), kind=kLoop, calls=%fused_computation.4 | loop fusion | flops 62873600 | bytes 84213760 | tf_op jit(solution)/shard_map/reduce_sum | solution.py:46
  516.0 33.2 %fusion.198.clone.5 = bf16[4,512,20,64]{1,3,2,0:T(8,128)(2,1)} fusion(f32[4,20,512,512]{2,3,1,0:T(8,128)} %get-tuple-element.69, f32[4,20,512]{2,1,0:T(8,128)S(1)} %get-tuple-element.68, bf16[3,4,512,20,64]{2,4,3,0,1:T(8,128)(2,1)} %convert_bitcast_fusion.1, f32[4,512,20]{1,2,0:T(8,128)S(1)} %bitcast.440), kind=kOutput, calls=%fused_computation.200.clone.clone.clone.clone.2 | convolution fusion | flops 2752512000 | bytes 94699520 | tf_op jit(solution)/shard_map/bhqk,bkhd->bqhd/dot_general | solution.py:47
  588.5 17.4 %convert_reduce_fusion.3 = (f32[4,512]{1,0:T(4,128)S(1)}, bf16[4,512,1280]{2,1,0:T(8,128)(2,1)}) fusion(f32[1280]{0:T(1024)S(1)} %copy-done.49, bf16[2,2,20,64,1280]{4,3,2,1,0:T(8,128)(2,1)} %param.36, f32[4,512,20]{1,2,0:T(8,128)S(1)} %bitcast.443, f32[4,20,512,77]{2,3,1,0:T(8,128)} %get-tuple-element.73, f32[4,20,512]{2,1,0:T(8,128)S(1)} %get-tuple-element.72, ...), kind=kOutput, calls=%fused_computation.86 | convolution fusion | flops 7145019392 | bytes 28590080 | tf_op jit(solution)/shard_map/bnhd,hdc->bnc/dot_general | solution.py:65
  610.0 70.1 %broadcast_add_fusion.1 = f32[4,512,10240]{2,1,0:T(8,128)} fusion(f32[10240]{0:T(1024)S(1)} %bitcast.445, bf16[2,1280,10240]{2,1,0:T(8,128)(2,1)} %param.38, bf16[4,512,1280]{2,1,0:T(8,128)(2,1)} %get-tuple-element.75, f32[1280]{0:T(1024)S(1)} %copy-done.35, f32[1280]{0:T(1024)S(1)} %copy-done.36, f32[4,512]{1,0:T(4,128)S(1)} %add_rsqrt_fusion.3, ...), kind=kOutput, calls=%fused_computation.48 | convolution fusion | flops 53723791360 | bytes 115410944 | tf_op jit(solution)/shard_map/bnc,cf->bnf/dot_general | solution.py:67
  680.0 129.2 %convert_reduce_fusion.2 = (f32[4,512]{1,0:T(4,128)S(1)}, bf16[4,512,1280]{2,1,0:T(8,128)(2,1)S(1)}) fusion(f32[1280]{0:T(1024)S(1)} %copy-done.43, bf16[2,5120,1280]{2,1,0:T(8,128)(2,1)} %param.40, f32[4,512,10240]{2,1,0:T(8,128)} %broadcast_add_fusion.1, bf16[4,512,1280]{2,1,0:T(8,128)(2,1)} %get-tuple-element.75), kind=kOutput, calls=%fused_computation.83 | convolution fusion | flops 27551332352 | bytes 107492352 | tf_op jit(solution)/shard_map/bnf,fc->bnc/dot_general | solution.py:69
  811.6 26.8 %convert_bitcast_fusion = bf16[3,4,512,20,64]{2,4,3,0,1:T(8,128)(2,1)} fusion(bf16[2,3,1280,20,64]{2,4,3,1,0:T(8,128)(2,1)} %param.33, bf16[4,512,1280]{2,1,0:T(8,128)(2,1)S(1)} %get-tuple-element.77, f32[1280]{0:T(1024)S(1)} %copy-done.33, f32[1280]{0:T(1024)S(1)} %copy-done.34, f32[4,512]{1,0:T(4,128)S(1)} %add_rsqrt_fusion.2, ...), kind=kOutput, calls=%fused_computation.80 | convolution fusion | flops 20156252160 | bytes 30828544 | tf_op jit(solution)/shard_map/bnc,jchd->jbnhd/dot_general | solution.py:58
  838.4 33.0 %multiply_reduce_fusion = (f32[4,20,512]{2,1,0:T(8,128)S(1)}, f32[4,20,512,512]{2,3,1,0:T(8,128)}) fusion(bf16[3,4,512,20,64]{2,4,3,0,1:T(8,128)(2,1)} %convert_bitcast_fusion), kind=kOutput, calls=%fused_computation.2 | convolution fusion | flops 2726256640 | bytes 94535680 | tf_op jit(solution)/shard_map/bqhd,bkhd->bhqk/dot_general | solution.py:44
  871.3 26.1 %fusion.2 = f32[4,20,512]{2,1,0:T(8,128)S(1)} fusion(f32[4,20,512,512]{2,3,1,0:T(8,128)} %get-tuple-element.79, f32[4,20,512]{2,1,0:T(8,128)S(1)} %get-tuple-element.78), kind=kLoop, calls=%fused_computation.6 | loop fusion | flops 62873600 | bytes 84213760 | tf_op jit(solution)/shard_map/reduce_sum | solution.py:46
  897.4 33.1 %fusion.204.clone.5 = bf16[4,512,20,64]{1,3,2,0:T(8,128)(2,1)} fusion(f32[4,20,512,512]{2,3,1,0:T(8,128)} %get-tuple-element.79, f32[4,20,512]{2,1,0:T(8,128)S(1)} %get-tuple-element.78, bf16[3,4,512,20,64]{2,4,3,0,1:T(8,128)(2,1)} %convert_bitcast_fusion, f32[4,512,20]{1,2,0:T(8,128)S(1)} %bitcast.441), kind=kOutput, calls=%fused_computation.194.clone.clone.clone.clone.2 | convolution fusion | flops 2752512000 | bytes 94699520 | tf_op jit(solution)/shard_map/bhqk,bkhd->bqhd/dot_general | solution.py:47
  969.6 17.4 %convert_reduce_fusion = (f32[4,512]{1,0:T(4,128)S(1)}, bf16[4,512,1280]{2,1,0:T(8,128)(2,1)}) fusion(f32[1280]{0:T(1024)S(1)} %copy-done.47, bf16[2,2,20,64,1280]{4,3,2,1,0:T(8,128)(2,1)} %param.36, f32[4,512,20]{1,2,0:T(8,128)S(1)} %bitcast.442, f32[4,20,512,77]{2,3,1,0:T(8,128)} %get-tuple-element.83, f32[4,20,512]{2,1,0:T(8,128)S(1)} %get-tuple-element.82, ...), kind=kOutput, calls=%fused_computation.76 | convolution fusion | flops 7145019392 | bytes 28590080 | tf_op jit(solution)/shard_map/bnhd,hdc->bnc/dot_general | solution.py:65
  991.3 70.4 %broadcast_add_fusion = f32[4,512,10240]{2,1,0:T(8,128)} fusion(f32[10240]{0:T(1024)S(1)} %bitcast.444, bf16[2,1280,10240]{2,1,0:T(8,128)(2,1)} %param.38, bf16[4,512,1280]{2,1,0:T(8,128)(2,1)} %get-tuple-element.85, f32[1280]{0:T(1024)S(1)} %copy-done.30, f32[1280]{0:T(1024)S(1)} %copy-done.29, f32[4,512]{1,0:T(4,128)S(1)} %add_rsqrt_fusion, ...), kind=kOutput, calls=%fused_computation.33 | convolution fusion | flops 53723791360 | bytes 115410944 | tf_op jit(solution)/shard_map/bnc,cf->bnf/dot_general | solution.py:67
  1061.7 128.5 %fusion.121 = bf16[4,512,1280]{2,1,0:T(8,128)(2,1)} fusion(bf16[4,512,1280]{2,1,0:T(8,128)(2,1)S(1)} %bitcast.438, bf16[2,5120,1280]{2,1,0:T(8,128)(2,1)} %param.40, f32[4,512,10240]{2,1,0:T(8,128)} %broadcast_add_fusion, f32[1280]{0:T(1024)S(1)} %copy-done.42), kind=kOutput, calls=%fused_computation.176 | convolution fusion | flops 27546091520 | bytes 107484160 | tf_op jit(solution)/shard_map/bnf,fc->bnc/dot_general | solution.py:69
  1223.9 134.9 %convert_multiply_fusion = (f32[8,32,9,1280]{3,1,2,0:T(8,128)}, bf16[8,32,9,1280]{3,1,2,0:T(8,128)(2,1)S(1)}) fusion(f32[8,32,9,1280]{3,0,2,1:T(8,128)} %bitcast.436, f32[1280]{0:T(1024)S(1)} %copy-done.46, bf16[2,2,3,3,1280,1280]{5,4,3,2,1,0:T(8,128)(2,1)} %param.25, bf16[8,4,8,11,1280]{4,0,3,2,1:T(8,128)(2,1)} %fusion.146, pred[32,9]{0,1:T(8,128)(4,1)S(1)} %copy-done.28), kind=kOutput, calls=%fused_computation.247 | convolution fusion | flops 62303109120 | bytes 66196768 | tf_op jit(solution)/shard_map/conv_general_dilated | solution.py:23
  1365.4 15.5 copy.112
  1403.9 83.9 %fusion.160 = f32[8,32,9,1280]{3,1,2,0:T(8,128)} fusion(bf16[2,2,3,3,1280,1280]{5,4,3,2,1,0:T(8,128)(2,1)} %param.25, f32[1280]{0:T(1024)S(1)} %copy-done.45, bf16[8,32,11,1280]{3,1,2,0:T(8,128)(2,1)S(1)} %fusion.467), kind=kOutput, calls=%fused_computation.225 | convolution fusion | flops 62288363520 | bytes 48501760 | tf_op jit(solution)/shard_map/conv_general_dilated | solution.py:23
  1487.9 15.6 copy.114
  1522.4 62.0 %all_to_all.27 = bf16[4,8,64,1280]{3,2,0,1:T(8,128)(2,1)S(1)} all-to-all(bf16[4,8,64,1280]{3,2,0,1:T(8,128)(2,1)S(1)} %copy.116), channel_id=1, replica_groups=mesh['dp'=2,'sp'=4] {'sp'}, dimensions={1} | all-to-all | bytes 10485760 | tf_op jit(solution)/shard_map/all_to_all | solution.py:83
  (254 shorter events, 324.9 us)
Async XLA Ops:
  0.0 65.4 %all-to-all-start = ((bf16[16,2,64,1280]{3,2,1,0:T(8,128)(2,1)}), bf16[16,2,64,1280]{3,2,1,0:T(8,128)(2,1)}, u32[]{:S(2)}, u32[]{:S(2)}) async-start(bf16[16,2,64,1280]{3,2,1,0:T(8,128)(2,1)} %param.21), calls=%async_computation | async-start | bytes 10485760 | tf_op jit(solution)/shard_map/all_to_all | solution.py:77
  13.5 14.9 slice-start.4
  515.9 33.2 %copy-start.50 = (f32[1280]{0:T(1024)S(1)}, f32[1280]{0:T(1024)}, u32[]{:S(2)}) copy-start(f32[1280]{0:T(1024)} %get-tuple-element.37) | copy-start | bytes 15364
  549.1 15.6 copy-start.37
  549.1 15.6 copy-start.38
  549.2 15.6 copy-start.54
  588.5 21.4 %copy-start.10 = (f32[1,10240]{1,0:T(1,128)S(1)}, f32[1,10240]{1,0:T(1,128)}, u32[]{:S(2)}) copy-start(f32[1,10240]{1,0:T(1,128)} %get-tuple-element.53) | copy-start | bytes 122884
  588.5 21.4 %copy-start.35 = (f32[1280]{0:T(1024)S(1)}, f32[1280]{0:T(1024)}, u32[]{:S(2)}) copy-start(f32[1280]{0:T(1024)} %get-tuple-element.16) | copy-start | bytes 15364
  588.5 21.4 %copy-start.36 = (f32[1280]{0:T(1024)S(1)}, f32[1280]{0:T(1024)}, u32[]{:S(2)}) copy-start(f32[1280]{0:T(1024)} %get-tuple-element.17) | copy-start | bytes 15364
  609.9 70.1 %copy-start.43 = (f32[1280]{0:T(1024)S(1)}, f32[1280]{0:T(1024)}, u32[]{:S(2)}) copy-start(f32[1280]{0:T(1024)} %get-tuple-element.42) | copy-start | bytes 15364
  680.0 131.6 %copy-start.33 = (f32[1280]{0:T(1024)S(1)}, f32[1280]{0:T(1024)}, u32[]{:S(2)}) copy-start(f32[1280]{0:T(1024)} %get-tuple-element.14) | copy-start | bytes 15364
  680.0 131.6 %copy-start.34 = (f32[1280]{0:T(1024)S(1)}, f32[1280]{0:T(1024)}, u32[]{:S(2)}) copy-start(f32[1280]{0:T(1024)} %get-tuple-element.15) | copy-start | bytes 15364
  897.4 33.1 %copy-start.48 = (f32[1280]{0:T(1024)S(1)}, f32[1280]{0:T(1024)}, u32[]{:S(2)}) copy-start(f32[1280]{0:T(1024)} %get-tuple-element.38) | copy-start | bytes 15364
  930.5 15.6 copy-start.31
  930.5 15.6 copy-start.32
  930.5 15.6 copy-start.53
  969.6 21.7 %copy-start.9 = (f32[1,10240]{1,0:T(1,128)S(1)}, f32[1,10240]{1,0:T(1,128)}, u32[]{:S(2)}) copy-start(f32[1,10240]{1,0:T(1,128)} %get-tuple-element.52) | copy-start | bytes 122884
  969.6 21.7 %copy-start.29 = (f32[1280]{0:T(1024)S(1)}, f32[1280]{0:T(1024)}, u32[]{:S(2)}) copy-start(f32[1280]{0:T(1024)} %get-tuple-element.11) | copy-start | bytes 15364
  969.6 21.7 %copy-start.30 = (f32[1280]{0:T(1024)S(1)}, f32[1280]{0:T(1024)}, u32[]{:S(2)}) copy-start(f32[1280]{0:T(1024)} %get-tuple-element.22) | copy-start | bytes 15364
  987.1 74.6 %slice-start.2 = ((s8[5242880]{0:T(1024)(128)(4,1)}), s8[4194304]{0:T(1024)(128)(4,1)S(1)}, s32[]{:S(2)}) async-start(s8[5242880]{0:T(1024)(128)(4,1)} %bitcast.437), calls=%async_computation.4 | async-start | bytes 8388608
  991.3 70.4 %slice-start.3 = ((s8[5242880]{0:T(1024)(128)(4,1)}), s8[1048576]{0:T(1024)(128)(4,1)S(1)}, s32[]{:S(2)}) async-start(s8[5242880]{0:T(1024)(128)(4,1)} %bitcast.437), calls=%async_computation.5 | async-start | bytes 2097152
  991.3 70.4 %copy-start.42 = (f32[1280]{0:T(1024)S(1)}, f32[1280]{0:T(1024)}, u32[]{:S(2)}) copy-start(f32[1280]{0:T(1024)} %get-tuple-element.41) | copy-start | bytes 15364
  1061.7 128.5 %copy-start.2 = (f32[4,8,64,1280]{3,2,1,0:T(8,128)S(1)}, f32[4,8,64,1280]{3,2,1,0:T(8,128)}, u32[]{:S(2)}) copy-start(f32[4,8,64,1280]{3,2,1,0:T(8,128)} %copy.106) | copy-start | bytes 31457284
  1061.7 128.5 %copy-start.41 = (f32[1280]{0:T(1024)S(1)}, f32[1280]{0:T(1024)}, u32[]{:S(2)}) copy-start(f32[1280]{0:T(1024)} %get-tuple-element.39) | copy-start | bytes 15364
  (41 other events, 290.2 us)

commit v2 on v1

v2 whole, which is shorter than its diff:
```python
import functools
import math
import jax
import jax.numpy as jnp
import numpy as np
from jax import lax
from jax.experimental import pallas as pl
from jax.experimental.pallas import tpu as pltpu
from jax.sharding import PartitionSpec as P

BF = jnp.bfloat16
F32 = jnp.float32
NUM_GROUPS = 32
WIDTH = 64
CBLK = 256
VMEM_CAP = 63 << 20


def mm(lhs, rhs):
    return jnp.dot(lhs, rhs, preferred_element_type=F32)


def split_rows(first, second):
    parts = []
    for row in (first, second):
        high = row.astype(BF).astype(F32)
        rest = row - high
        mid = rest.astype(BF).astype(F32)
        parts += [high, mid, rest - mid]
    parts += [jnp.zeros_like(first)] * 2
    return jnp.concatenate(parts, 0).astype(BF)


def group_tables(chan_n):
    member = np.zeros((chan_n, 128), np.float32)
    member[np.arange(chan_n), np.arange(chan_n) // (chan_n // NUM_GROUPS)] = 1.0
    return jnp.asarray(member, BF), jnp.asarray(member.T, BF)


def group_scale(chan_sum, chan_sq, to_group, to_chan, count_n, eps_val):
    sums = mm(split_rows(chan_sum, chan_sq), to_group)
    mean = (sums[0:1] + sums[1:2] + sums[2:3]) / count_n
    square = (sums[3:4] + sums[4:5] + sums[5:6]) / count_n
    inv_std = lax.rsqrt(square - mean * mean + eps_val)
    wide = mm(split_rows(mean, inv_std), to_chan)
    return wide[0:1] + wide[1:2] + wide[2:3], wide[3:4] + wide[4:5] + wide[5:6]


def latent_stats(src_ref):
    rows_n, chan_n = src_ref.shape
    sums, squares = [], []
    for col in range(0, chan_n, CBLK):
        part_sum, part_sq = 0.0, 0.0
        for row in range(0, rows_n, WIDTH):
            blk = src_ref[row:row + WIDTH, col:col + CBLK].astype(F32)
            blk = blk.reshape(WIDTH // 8, 8, CBLK)
            part_sum = part_sum + blk.sum(0)
            part_sq = part_sq + (blk * blk).sum(0)
        sums.append(part_sum.sum(0, keepdims=True))
        squares.append(part_sq.sum(0, keepdims=True))
    return jnp.concatenate(sums, 1), jnp.concatenate(squares, 1)


def silu(val):
    half = 0.5 * val
    return half + half * jnp.tanh(half)


def norm_latent(src_ref, dst_ref, gain, bias, to_group, to_chan, eps_val, spread):
    rows_n, chan_n = src_ref.shape
    chan_sum, chan_sq = latent_stats(src_ref)
    mean, inv_std = group_scale(chan_sum, chan_sq, to_group, to_chan, rows_n * (chan_n // NUM_GROUPS), eps_val)
    scale = inv_std * gain
    col_pos = lax.broadcasted_iota(jnp.int32, (WIDTH, CBLK), 0)
    for row in range(0, rows_n, WIDTH):
        for col in range(0, chan_n, CBLK):
            cols = slice(col, col + CBLK)
            val = (src_ref[row:row + WIDTH, cols].astype(F32) - mean[:, cols]) * scale[:, cols] + bias[:, cols]
            rows = slice(row, row + WIDTH)
            if not spread:
                dst_ref[rows, cols] = val.astype(BF)
                continue
            act = silu(val)
            before = jnp.where(col_pos == 0, 0.0, pltpu.roll(act, 1, 0))
            after = jnp.where(col_pos == WIDTH - 1, 0.0, pltpu.roll(act, WIDTH - 1, 0))
            dst_ref[rows, cols] = before.astype(BF)
            dst_ref[rows, chan_n + col:chan_n + col + CBLK] = act.astype(BF)
            dst_ref[rows, 2 * chan_n + col:2 * chan_n + col + CBLK] = after.astype(BF)


def affine(norm_ref, at):
    return norm_ref[at + (slice(0, 1),)], norm_ref[at + (slice(1, 2),)]


def prep_kernel(x_ref, norm_ref, tog_ref, toc_ref, o_ref, *, eps_val, at):
    norm_latent(x_ref, o_ref, *affine(norm_ref, at), tog_ref[...], toc_ref[...], eps_val, True)


HBM_SPEC = pl.BlockSpec(memory_space=pl.ANY)


def params():
    return pltpu.CompilerParams(vmem_limit_bytes=VMEM_CAP)


def whole(shape):
    return pl.BlockSpec(shape, lambda *_: (0,) * len(shape), pipeline_mode=pl.Buffered(1))


def prep_call(x, norm, at, eps_val):
    lat_n, rows_n, chan_n = x.shape
    to_group, to_chan = group_tables(chan_n)
    return pl.pallas_call(
        functools.partial(prep_kernel, eps_val=eps_val, at=at),
        grid=(lat_n,),
        in_specs=[pl.BlockSpec((None, rows_n, chan_n), lambda i: (i, 0, 0)), whole(norm.shape), whole((chan_n, 128)), whole((128, chan_n))],
        out_specs=pl.BlockSpec((None, rows_n, 3 * chan_n), lambda i: (i, 0, 0)),
        out_shape=jax.ShapeDtypeStruct((lat_n, rows_n, 3 * chan_n), BF),
        compiler_params=params(),
        name='prep',
    )(x, norm, to_group, to_chan)


def conv_kernel(*refs, lat_n, slot, eps_val, timed, residual, spread, normed, at):
    refs = list(refs)
    x3_ref, w_hbm, cb_ref = refs[:3]
    refs = refs[3:]
    time_ref = refs.pop(0) if timed else None
    res_ref = refs.pop(0) if residual else None
    if normed:
        norm_ref, tog_ref, toc_ref = refs[:3]
        refs = refs[3:]
    out_ref = refs.pop(0) if residual else None
    nrm_ref = refs.pop(0) if normed else None
    w_buf, sems, held = refs
    rows_n, chan_n = held.shape
    step = pl.program_id(0)
    third = 3 * chan_n

    parts = [(third + i * chan_n, chan_n) for i in range(3)] + [(0, third), (2 * third, third)]

    def fetch(i):
        first, size = parts[i]
        return pltpu.make_async_copy(w_hbm.at[slot, pl.ds(first, size)], w_buf.at[pl.ds(first, size)], sems.at[i])

    def convolve(first_time):
        def ready(i):
            if first_time:
                fetch(i).wait()
        if first_time:
            ready(0)
            mid = mm(x3_ref[:, 0:chan_n], w_buf[third:third + chan_n])
            ready(1)
            mid = mid + mm(x3_ref[:, chan_n:2 * chan_n], w_buf[third + chan_n:third + 2 * chan_n])
            ready(2)
            mid = mid + mm(x3_ref[:, 2 * chan_n:], w_buf[third + 2 * chan_n:2 * third])
        else:
            mid = mm(x3_ref[...], w_buf[third:2 * third])
        ready(3)
        upper = mm(x3_ref[0:rows_n - WIDTH, :], w_buf[0:third])
        ready(4)
        lower = mm(x3_ref[WIDTH:rows_n, :], w_buf[2 * third:3 * third])
        last = rows_n - WIDTH
        for rows, val in (
            (slice(0, WIDTH), mid[0:WIDTH] + lower[0:WIDTH]),
            (slice(WIDTH, last), mid[WIDTH:last] + upper[0:last - WIDTH] + lower[WIDTH:last]),
            (slice(last, rows_n), mid[last:] + upper[last - WIDTH:]),
        ):
            val = val + cb_ref[slot // 2, slot % 2:slot % 2 + 1, :]
            if timed:
                val = val + time_ref[...]
            if residual:
                val = res_ref[rows, :].astype(F32) + val
            val = val.astype(BF)
            if normed:
                held[rows, :] = val
            if residual:
                out_ref[rows, :] = val

    def finish():
        norm_latent(held, nrm_ref, *affine(norm_ref, at), tog_ref[...], toc_ref[...], eps_val, spread)

    @pl.when(step == 0)
    def _():
        for i in range(len(parts)):
            fetch(i).start()
        convolve(True)

    @pl.when((step > 0) & (step < lat_n))
    def _():
        if normed:
            finish()
        convolve(False)

    if normed:
        @pl.when(step == lat_n)
        def _():
            finish()


def conv_call(x3, w_all, slot, conv_b, time_row, res, norm, at, eps_val, spread):
    lat_n, rows_n, wide = x3.shape
    chan_n = wide // 3
    timed, residual, normed = time_row is not None, res is not None, norm is not None
    here = lambda i: (jnp.minimum(i, lat_n - 1), 0, 0)
    prev = lambda i: (jnp.maximum(i - 1, 0), 0, 0)
    args = [x3, w_all, conv_b]
    in_specs = [pl.BlockSpec((None, rows_n, wide), here), HBM_SPEC, whole(conv_b.shape)]
    out_specs, out_shape = [], []
    if timed:
        args.append(time_row)
        in_specs.append(pl.BlockSpec((None, 1, chan_n), here))
    if residual:
        args.append(res)
        in_specs.append(pl.BlockSpec((None, rows_n, chan_n), here))
        out_specs.append(pl.BlockSpec((None, rows_n, chan_n), here))
        out_shape.append(jax.ShapeDtypeStruct((lat_n, rows_n, chan_n), BF))
    if normed:
        to_group, to_chan = group_tables(chan_n)
        args += [norm, to_group, to_chan]
        in_specs += [whole(norm.shape), whole((chan_n, 128)), whole((128, chan_n))]
        out_n = wide if spread else chan_n
        out_specs.append(pl.BlockSpec((None, rows_n, out_n), prev))
        out_shape.append(jax.ShapeDtypeStruct((lat_n, rows_n, out_n), BF))
    flops = 2 * lat_n * rows_n * chan_n * wide * 3
    outs = pl.pallas_call(
        functools.partial(conv_kernel, lat_n=lat_n, slot=slot, eps_val=eps_val, timed=timed, residual=residual, spread=spread, normed=normed, at=at),
        grid=(lat_n + (1 if normed else 0),),
        in_specs=in_specs, out_specs=out_specs, out_shape=out_shape,
        scratch_shapes=[pltpu.VMEM((3 * wide, chan_n), BF), pltpu.SemaphoreType.DMA((5,)), pltpu.VMEM((rows_n, chan_n), BF)],
        compiler_params=params(),
        cost_estimate=pl.CostEstimate(flops=flops, bytes_accessed=3 * wide * chan_n * 2, transcendentals=0),
        name='conv',
    )(*args)
    return outs


LN_ROWS = 32
LOG2E = math.log2(math.e)


def mm_t(lhs, rhs):
    return lax.dot_general(lhs, rhs, (((1,), (1,)), ((), ())), preferred_element_type=F32)


def norm_rows(src_ref, dst_ref, gain, bias):
    for row in range(0, src_ref.shape[0], LN_ROWS):
        rows = slice(row, row + LN_ROWS)
        val = src_ref[rows, :].astype(F32)
        val = val - val.mean(-1, keepdims=True)
        var = (val * val).mean(-1, keepdims=True)
        dst_ref[rows, :] = (val * lax.rsqrt(var + 1e-5) * gain + bias).astype(BF)


def lat_spec(shape, lat_n, lag):
    return pl.BlockSpec((None,) + shape, lambda i: (jnp.clip(i - lag, 0, lat_n - 1),) + (0,) * len(shape))


def enter_kernel(n_ref, pw_hbm, pb_ref, ln_ref, qw_hbm, u_ref, qkv_ref, pw_buf, qw_buf, held, nrm, sems, *, lat_n, layer):
    step = pl.program_id(0)
    chan_n = held.shape[1]
    half = chan_n // 2
    copies = [pltpu.make_async_copy(pw_hbm.at[0, pl.ds(i * half, half)], pw_buf.at[pl.ds(i * half, half)], sems.at[i]) for i in range(2)]
    copies += [pltpu.make_async_copy(qw_hbm.at[layer, j], qw_buf.at[j], sems.at[2 + j]) for j in range(3)]

    def project(first):
        if first:
            copies[0].wait()
            val = mm(n_ref[:, 0:half], pw_buf[0:half])
            copies[1].wait()
            val = val + mm(n_ref[:, half:], pw_buf[half:])
        else:
            val = mm(n_ref[...], pw_buf[...])
        val = (val + pb_ref[0:1, :]).astype(BF)
        held[...] = val
        u_ref[...] = val

    def norm():
        norm_rows(held, nrm, *affine(ln_ref, (layer, 0)))

    def heads(first=False):
        for j in range(3):
            if first:
                copies[2 + j].wait()
            qkv_ref[:, j * chan_n:(j + 1) * chan_n] = mm_t(nrm[...], qw_buf[j]).astype(BF)

    @pl.when(step == 0)
    def _():
        for cp in copies:
            cp.start()
        project(True)

    @pl.when(step == 1)
    def _():
        norm()
        project(False)

    @pl.when(step == 2)
    def _():
        heads(True)
        norm()
        project(False)

    @pl.when((step > 2) & (step < lat_n))
    def _():
        heads()
        norm()
        project(False)

    @pl.when(step == lat_n)
    def _():
        heads()
        norm()

    @pl.when(step == lat_n + 1)
    def _():
        heads()


def enter_call(nrm_in, proj_w, proj_b, ln_par, qkv_t, layer):
    lat_n, rows_n, chan_n = nrm_in.shape
    return pl.pallas_call(
        functools.partial(enter_kernel, lat_n=lat_n, layer=layer),
        grid=(lat_n + 2,),
        in_specs=[lat_spec((rows_n, chan_n), lat_n, 0), HBM_SPEC, whole(proj_b.shape), whole(ln_par.shape), HBM_SPEC],
        out_specs=[lat_spec((rows_n, chan_n), lat_n, 0), lat_spec((rows_n, 3 * chan_n), lat_n, 2)],
        out_shape=[jax.ShapeDtypeStruct((lat_n, rows_n, chan_n), BF), jax.ShapeDtypeStruct((lat_n, rows_n, 3 * chan_n), BF)],
        scratch_shapes=[pltpu.VMEM((chan_n, chan_n), BF), pltpu.VMEM((3, chan_n, chan_n), BF), pltpu.VMEM((rows_n, chan_n), BF), pltpu.VMEM((rows_n, chan_n), BF), pltpu.SemaphoreType.DMA((5,))],
        compiler_params=params(),
        cost_estimate=pl.CostEstimate(flops=8 * lat_n * rows_n * chan_n * chan_n, bytes_accessed=8 * chan_n * chan_n, transcendentals=0),
        name='enter',
    )(nrm_in, proj_w, proj_b, ln_par, qkv_t)


def heads_kernel(u_ref, ln_ref, qw_hbm, qkv_ref, qw_buf, nrm, sems, *, lat_n, layer):
    step = pl.program_id(0)
    chan_n = nrm.shape[1]
    copies = [pltpu.make_async_copy(qw_hbm.at[layer, j], qw_buf.at[j], sems.at[j]) for j in range(3)]

    def norm():
        norm_rows(u_ref, nrm, *affine(ln_ref, (layer, 0)))

    def heads(first=False):
        for j in range(3):
            if first:
                copies[j].wait()
            qkv_ref[:, j * chan_n:(j + 1) * chan_n] = mm_t(nrm[...], qw_buf[j]).astype(BF)

    @pl.when(step == 0)
    def _():
        for cp in copies:
            cp.start()
        norm()

    @pl.when(step == 1)
    def _():
        heads(True)
        norm()

    @pl.when((step > 1) & (step < lat_n))
    def _():
        heads()
        norm()

    @pl.when(step == lat_n)
    def _():
        heads()


def heads_call(u, ln_par, qkv_t, layer):
    lat_n, rows_n, chan_n = u.shape
    return pl.pallas_call(
        functools.partial(heads_kernel, lat_n=lat_n, layer=layer),
        grid=(lat_n + 1,),
        in_specs=[lat_spec((rows_n, chan_n), lat_n, 0), whole(ln_par.shape), HBM_SPEC],
        out_specs=lat_spec((rows_n, 3 * chan_n), lat_n, 1),
        out_shape=jax.ShapeDtypeStruct((lat_n, rows_n, 3 * chan_n), BF),
        scratch_shapes=[pltpu.VMEM((3, chan_n, chan_n), BF), pltpu.VMEM((rows_n, chan_n), BF), pltpu.SemaphoreType.DMA((3,))],
        compiler_params=params(),
        cost_estimate=pl.CostEstimate(flops=6 * lat_n * rows_n * chan_n * chan_n, bytes_accessed=6 * chan_n * chan_n, transcendentals=0),
        name='heads',
    )(u, ln_par, qkv_t)


HEAD_DIM = 64
PAIR = 2 * HEAD_DIM
EXP_SCALE = LOG2E / math.sqrt(HEAD_DIM)


def attn_kernel(q_ref, k_ref, v_ref, o_ref, *, q_rows):
    rows_n, chan_n = q_ref.shape
    left = lax.broadcasted_iota(jnp.int32, (q_rows, PAIR), 1) < HEAD_DIM

    def scores(unit):
        cols, rows = unit
        q = q_ref[rows, cols]
        zero = jnp.zeros_like(q)
        return mm_t(jnp.where(left, q, zero), k_ref[:, cols]), mm_t(jnp.where(left, zero, q), k_ref[:, cols])

    def finish(unit, pair):
        cols, rows = unit
        outs = []
        for s in pair:
            e = jnp.exp2((s - s.max(-1, keepdims=True)) * EXP_SCALE)
            outs.append(mm(e.astype(BF), v_ref[:, cols]) / e.sum(-1, keepdims=True))
        o_ref[rows, cols] = jnp.where(left, outs[0], outs[1]).astype(BF)

    units = [(slice(c, c + PAIR), slice(r, r + q_rows)) for c in range(0, chan_n, PAIR) for r in range(0, rows_n, q_rows)]
    waiting = None
    for unit in units:
        pair = scores(unit)
        if waiting is not None:
            finish(*waiting)
        waiting = (unit, pair)
    finish(*waiting)


def attn_call(qkv):
    lat_n, rows_n, wide = qkv.shape
    chan_n = wide // 3
    return pl.pallas_call(
        functools.partial(attn_kernel, q_rows=256),
        grid=(lat_n,),
        in_specs=[pl.BlockSpec((None, rows_n, chan_n), lambda i, j=j: (i, 0, j)) for j in range(3)],
        out_specs=pl.BlockSpec((None, rows_n, chan_n), lambda i: (i, 0, 0)),
        out_shape=jax.ShapeDtypeStruct((lat_n, rows_n, chan_n), BF),
        compiler_params=params(),
        cost_estimate=pl.CostEstimate(flops=16 * lat_n * rows_n * rows_n * chan_n, bytes_accessed=8 * lat_n * rows_n * chan_n, transcendentals=0),
        name='attn',
    )(qkv, qkv, qkv)


KEY_PAD = 128


def mix_kernel(o_ref, u_ref, kc_ref, vc_ref, ow_hbm, ob_ref, qw_hbm, ln_ref, u_out, n_out, ow_buf, cw_buf, qw_buf, mid, mid_old, nrm, crossed, sems, *, lat_n, layer, key_n):
    step = pl.program_id(0)
    rows_n, chan_n = mid.shape
    copies = [pltpu.make_async_copy(ow_hbm.at[layer, 0], ow_buf, sems.at[0]), pltpu.make_async_copy(qw_hbm.at[layer], qw_buf, sems.at[1]), pltpu.make_async_copy(ow_hbm.at[layer, 1], cw_buf, sems.at[2])]

    def leave(first=False):
        if first:
            copies[2].wait()
        val = mid_old[...].astype(F32) + (mm(crossed[...], cw_buf[...]) + ob_ref[layer, 1:2, :])
        u_out[...] = val.astype(BF)
        norm_rows(u_out, n_out, *affine(ln_ref, (layer, 2)))

    def cross(first=False):
        if first:
            copies[1].wait()
        q_all = mm_t(nrm[...], qw_buf[...]).astype(BF)
        key_rows = kc_ref.shape[0]
        key_left = lax.broadcasted_iota(jnp.int32, (key_rows, PAIR), 1) < HEAD_DIM
        valid = lax.broadcasted_iota(jnp.int32, (rows_n, KEY_PAD), 1) < key_n
        left = lax.broadcasted_iota(jnp.int32, (rows_n, PAIR), 1) < HEAD_DIM
        zero = jnp.zeros((key_rows, PAIR), BF)
        fill = jnp.zeros((KEY_PAD - key_rows, PAIR), BF)
        for col in range(0, chan_n, PAIR):
            cols = slice(col, col + PAIR)
            keys, vals = kc_ref[:, cols], vc_ref[:, cols]
            keys = jnp.concatenate([jnp.where(key_left, keys, zero), fill, jnp.where(key_left, zero, keys), fill], 0)
            vals = jnp.concatenate([jnp.where(key_left, vals, zero), fill, jnp.where(key_left, zero, vals), fill], 0)
            s = mm_t(q_all[:, cols], keys)
            exps, sums = [], []
            for h in range(2):
                sh = jnp.where(valid, s[:, h * KEY_PAD:(h + 1) * KEY_PAD], -jnp.inf)
                e = jnp.exp2((sh - sh.max(-1, keepdims=True)) * EXP_SCALE)
                exps.append(e.astype(BF))
                sums.append(e.sum(-1, keepdims=True))
            got = mm(jnp.concatenate(exps, 1), vals)
            crossed[:, cols] = (got / jnp.where(left, sums[0], sums[1])).astype(BF)
        mid_old[...] = mid[...]

    def arrive(first=False):
        if first:
            copies[0].wait()
        val = u_ref[...].astype(F32) + (mm(o_ref[...], ow_buf[...]) + ob_ref[layer, 0:1, :])
        mid[...] = val.astype(BF)
        norm_rows(mid, nrm, *affine(ln_ref, (layer, 1)))

    @pl.when(step == 0)
    def _():
        for cp in copies:
            cp.start()
        arrive(True)

    @pl.when(step == 1)
    def _():
        cross(True)
        arrive()

    @pl.when(step == 2)
    def _():
        leave(True)
        cross()
        arrive()

    @pl.when((step > 2) & (step < lat_n))
    def _():
        leave()
        cross()
        arrive()

    @pl.when(step == lat_n)
    def _():
        leave()
        cross()

    @pl.when(step == lat_n + 1)
    def _():
        leave()


def mix_call(o, u, kv, key_n, out_w, out_b, q_t, ln_par, layer):
    lat_n, rows_n, chan_n = u.shape
    blk = (rows_n, chan_n)

    def kv_spec(j):
        return pl.BlockSpec((None, None, None, kv.shape[3], chan_n), lambda i: (layer, j, jnp.clip(i - 1, 0, lat_n - 1), 0, 0))

    return pl.pallas_call(
        functools.partial(mix_kernel, lat_n=lat_n, layer=layer, key_n=key_n),
        grid=(lat_n + 2,),
        in_specs=[lat_spec(blk, lat_n, 0), lat_spec(blk, lat_n, 0), kv_spec(0), kv_spec(1), HBM_SPEC, whole(out_b.shape), HBM_SPEC, whole(ln_par.shape)],
        out_specs=[lat_spec(blk, lat_n, 2), lat_spec(blk, lat_n, 2)],
        out_shape=[jax.ShapeDtypeStruct((lat_n,) + blk, BF)] * 2,
        scratch_shapes=[pltpu.VMEM((chan_n, chan_n), BF)] * 3 + [pltpu.VMEM(blk, BF)] * 4 + [pltpu.SemaphoreType.DMA((3,))],
        compiler_params=params(),
        cost_estimate=pl.CostEstimate(flops=6 * lat_n * rows_n * chan_n * chan_n, bytes_accessed=6 * chan_n * chan_n, transcendentals=0),
        name='mix',
    )(o, u, kv, kv, out_w, out_b, q_t, ln_par)


def gelu(val):
    return 0.5 * val * (1.0 + lax.erf(val * math.sqrt(0.5)))


def ff_kernel(n_hbm, r_hbm, wa_ref, wb_ref, ba_ref, bb_ref, wo_ref, bo_ref, o_hbm, n_buf, r_buf, pa, pb, gate, acc, in_sems, r_sem, out_sems, *, steps, chunk, layer):
    step = pl.program_id(0)
    tok_n = n_buf.shape[0]
    pieces = [pl.ds(i * chunk, chunk) for i in range(tok_n // chunk)]
    loads = [pltpu.make_async_copy(n_hbm.at[p], n_buf.at[p], in_sems.at[i]) for i, p in enumerate(pieces)]
    r_load = pltpu.make_async_copy(r_hbm, r_buf, r_sem)
    stores = [pltpu.make_async_copy(r_buf.at[p], o_hbm.at[p], out_sems.at[i]) for i, p in enumerate(pieces)]

    def widen(first=False):
        for i, p in enumerate(pieces):
            if first:
                loads[i].wait()
            pa[p, :] = mm(n_buf[p, :], wa_ref[...])
            pb[p, :] = mm(n_buf[p, :], wb_ref[...])

    def activate():
        for p in pieces:
            gate[p, :] = ((pa[p, :] + ba_ref[layer:layer + 1, :]) * gelu(pb[p, :] + bb_ref[layer:layer + 1, :])).astype(BF)

    def narrow(first=False):
        for p in pieces:
            val = mm(gate[p, :], wo_ref[...])
            if first:
                acc[p, :] = val
            else:
                acc[p, :] += val

    @pl.when(step == 0)
    def _():
        for cp in loads:
            cp.start()
        widen(True)

    @pl.when(step == 1)
    def _():
        r_load.start()
        activate()
        widen()

    @pl.when(step == 2)
    def _():
        narrow(True)
        activate()
        widen()

    @pl.when((step > 2) & (step < steps))
    def _():
        narrow()
        activate()
        widen()

    @pl.when(step == steps)
    def _():
        narrow()
        activate()

    @pl.when(step == steps + 1)
    def _():
        r_load.wait()
        for i, p in enumerate(pieces):
            val = acc[p, :] + mm(gate[p, :], wo_ref[...]) + bo_ref[layer:layer + 1, :]
            r_buf[p, :] = (r_buf[p, :].astype(F32) + val).astype(BF)
            stores[i].start()
        for cp in stores:
            cp.wait()


def ff_call(nrm, res, w_in, b_in, w_out, b_out, layer, fb=512, chunk=512):
    tok_n, chan_n = nrm.shape
    ff_n = w_out.shape[1]
    steps = ff_n // fb
    now = lambda s: jnp.minimum(s, steps - 1)
    act = lambda s: jnp.clip(s - 1, 0, steps - 1)
    return pl.pallas_call(
        functools.partial(ff_kernel, steps=steps, chunk=chunk, layer=layer),
        grid=(steps + 2,),
        in_specs=[HBM_SPEC, HBM_SPEC,
                  pl.BlockSpec((None, chan_n, fb), lambda s: (layer, 0, now(s))),
                  pl.BlockSpec((None, chan_n, fb), lambda s: (layer, 0, steps + now(s))),
                  pl.BlockSpec((b_in.shape[0], fb), lambda s: (0, act(s))),
                  pl.BlockSpec((b_in.shape[0], fb), lambda s: (0, steps + act(s))),
                  pl.BlockSpec((None, fb, chan_n), lambda s: (layer, jnp.maximum(s - 2, 0), 0)),
                  whole(b_out.shape)],
        out_specs=HBM_SPEC,
        out_shape=jax.ShapeDtypeStruct((tok_n, chan_n), BF),
        scratch_shapes=[pltpu.VMEM((tok_n, chan_n), BF)] * 2 + [pltpu.VMEM((tok_n, fb), F32)] * 2 + [pltpu.VMEM((tok_n, fb), BF), pltpu.VMEM((tok_n, chan_n), F32), pltpu.SemaphoreType.DMA((tok_n // chunk,)), pltpu.SemaphoreType.DMA, pltpu.SemaphoreType.DMA((tok_n // chunk,))],
        compiler_params=params(),
        cost_estimate=pl.CostEstimate(flops=6 * tok_n * chan_n * ff_n, bytes_accessed=6 * chan_n * ff_n, transcendentals=0),
        name='ff',
    )(nrm, res, w_in, w_in, b_in, b_in, w_out, b_out)


def exit_kernel(u_ref, h_ref, pw_hbm, pb_ref, norm_ref, tog_ref, toc_ref, m_ref, x_ref, pw_buf, held, sems, *, lat_n, eps_val, at):
    step = pl.program_id(0)
    chan_n = held.shape[1]
    half = chan_n // 2
    copies = [pltpu.make_async_copy(pw_hbm.at[1, pl.ds(i * half, half)], pw_buf.at[pl.ds(i * half, half)], sems.at[i]) for i in range(2)]

    def project(first=False):
        if first:
            copies[0].wait()
            val = mm(u_ref[:, 0:half], pw_buf[0:half])
            copies[1].wait()
            val = val + mm(u_ref[:, half:], pw_buf[half:])
        else:
            val = mm(u_ref[...], pw_buf[...])
        val = (val + pb_ref[1:2, :] + h_ref[...].astype(F32)).astype(BF)
        held[...] = val
        m_ref[...] = val

    def finish():
        norm_latent(held, x_ref, *affine(norm_ref, at), tog_ref[...], toc_ref[...], eps_val, True)

    @pl.when(step == 0)
    def _():
        for cp in copies:
            cp.start()
        project(True)

    @pl.when((step > 0) & (step < lat_n))
    def _():
        finish()
        project()

    @pl.when(step == lat_n)
    def _():
        finish()


def exit_call(u, h, proj_w, proj_b, norm, at, eps_val):
    lat_n, rows_n, chan_n = u.shape
    to_group, to_chan = group_tables(chan_n)
    blk = (rows_n, chan_n)
    return pl.pallas_call(
        functools.partial(exit_kernel, lat_n=lat_n, eps_val=eps_val, at=at),
        grid=(lat_n + 1,),
        in_specs=[lat_spec(blk, lat_n, 0), lat_spec(blk, lat_n, 0), HBM_SPEC, whole(proj_b.shape), whole(norm.shape), whole((chan_n, 128)), whole((128, chan_n))],
        out_specs=[lat_spec(blk, lat_n, 0), lat_spec((rows_n, 3 * chan_n), lat_n, 1)],
        out_shape=[jax.ShapeDtypeStruct((lat_n,) + blk, BF), jax.ShapeDtypeStruct((lat_n, rows_n, 3 * chan_n), BF)],
        scratch_shapes=[pltpu.VMEM((chan_n, chan_n), BF), pltpu.VMEM(blk, BF), pltpu.SemaphoreType.DMA((2,))],
        compiler_params=params(),
        cost_estimate=pl.CostEstimate(flops=2 * lat_n * rows_n * chan_n * chan_n, bytes_accessed=2 * chan_n * chan_n, transcendentals=0),
        name='exit',
    )(u, h, proj_w, proj_b, norm, to_group, to_chan)


def device_block(latents, time_emb, context, res_norm, res_conv_w, res_conv_b, res_temb_w, res_temb_b, tr_norm, proj_w, proj_b, ln_par, self_qkv, cross_q, cross_kv, attn_out, attn_b, ff_in_w, ff_in_b, ff_out_w, ff_out_b, sp_size):
    lat_all, band_n, width_n, chan_n = latents.shape
    own_n = lat_all // sp_size
    tok_n = band_n * sp_size * width_n
    first = lax.axis_index('sp') * own_n
    whole_lat = lax.all_to_all(latents, 'sp', 0, 1, tiled=True).reshape(own_n, tok_n, chan_n)
    time_own = lax.dynamic_slice_in_dim(time_emb, first, own_n, 0)
    ctx_own = lax.dynamic_slice_in_dim(context, first, own_n, 0)
    key_n = ctx_own.shape[1]
    ctx_pad = jnp.pad(ctx_own, ((0, 0), (0, -key_n % 16), (0, 0)))

    conv_w = res_conv_w.reshape(4, 9 * chan_n, chan_n)
    qkv_t = self_qkv.transpose(0, 1, 3, 4, 2).reshape(2, 3, chan_n, chan_n)
    cross_q_t = cross_q.transpose(0, 2, 3, 1).reshape(2, chan_n, chan_n)
    cross_kv_t = cross_kv.transpose(0, 1, 3, 4, 2).reshape(2, 2, chan_n, -1)
    out_w = attn_out.reshape(2, 2, chan_n, chan_n)
    trunk_norm = tr_norm[None]

    kv = jnp.einsum('btc,ljdc->ljbtd', ctx_pad, cross_kv_t, preferred_element_type=F32).astype(BF)
    time_act = jax.nn.silu(time_own.astype(F32)).astype(BF)
    time_rows = [(jnp.dot(time_act, res_temb_w[r], preferred_element_type=F32) + res_temb_b[r])[:, None, :] for r in range(2)]

    spread = prep_call(whole_lat, res_norm, (0, 0), 1e-5)
    spread, = conv_call(spread, conv_w, 0, res_conv_b, time_rows[0], None, res_norm, (0, 1), 1e-5, True)
    hidden, normed = conv_call(spread, conv_w, 1, res_conv_b, None, whole_lat, trunk_norm, (0,), 1e-6, False)
    for layer in range(2):
        if layer == 0:
            tokens, qkv = enter_call(normed, proj_w, proj_b, ln_par, qkv_t, 0)
        else:
            qkv = heads_call(tokens, ln_par, qkv_t, layer)
        attended = attn_call(qkv)
        tokens, normed = mix_call(attended, tokens, kv, key_n, out_w, attn_b, cross_q_t, ln_par, layer)
        flat = (own_n * tok_n, chan_n)
        tokens = ff_call(normed.reshape(flat), tokens.reshape(flat), ff_in_w, ff_in_b, ff_out_w, ff_out_b, layer).reshape(own_n, tok_n, chan_n)
    middle, spread = exit_call(tokens, hidden, proj_w, proj_b, res_norm, (1, 0), 1e-5)
    spread, = conv_call(spread, conv_w, 2, res_conv_b, time_rows[1], None, res_norm, (1, 1), 1e-5, True)
    last, = conv_call(spread, conv_w, 3, res_conv_b, None, middle, None, None, 0.0, False)
    return lax.all_to_all(last.reshape(own_n, band_n * sp_size, width_n, chan_n), 'sp', 1, 0, tiled=True)


def solution(mesh):
    sp_size = mesh.shape['sp']
    row_spec = P('dp', 'sp')
    part_spec = P('dp')
    in_specs = (row_spec, part_spec, part_spec) + (P(),) * 18
    body_fn = functools.partial(device_block, sp_size=sp_size)
    return jax.shard_map(body_fn, mesh=mesh, in_specs=in_specs, out_specs=row_spec, check_vma=False)
```

time: 1600 us -> 988 us (0.62)
  matrix products: 1160 us -> 15.5 us
  Pallas kernels: 0 us -> 843 us
  other arithmetic: 188 us -> 0 us
  local copies, waits for them, and re-layouts: 147 us -> 15.4 us
    pallas_call x0 -> x14, Pallas kernels: none -> 843 us  [the longest x4 328 us: conv_call(): pl.pallas_call(functools.partial(conv_kernel, lat_n=lat_n, slot=slot, eps...]
    dot_general x22 -> x3, matrix products: 717 us -> 15.5 us  [the longest x1 12.3 us: device_block(): jnp.einsum('btc,ljdc->ljbtd', ctx_pad, cross_kv_t, preferred_element_type...]
    conv_general_dilated x4 -> x0, matrix products: 438 us -> none  [conv_rows(): lax.conv_general_dilated(act_in, kernel, (1, 1), ((1, 1), (1, 1)), dimens...]
    reduce_sum x26 -> x0, other arithmetic: 113 us -> none  [the longest x4 69.1 us: attend_block(): row_sum = row_exp.sum(axis=-1)]
    convert_element_type x7 -> x0, other arithmetic: 60.4 us -> none  [the longest x2 21.8 us: resnet_local(): jax.nn.silu(group_norm(hidden, res_norm[res_index, 1, 0], res_norm[res_in...]
    convert_element_type x11 -> x0, local copies, waits for them, and re-layouts: 46.1 us -> none  [the longest x3 26.5 us: resnet_local(): return (latents.astype(jnp.float32) + update).astype(jnp.bfloat16)]
    add x4 -> x0, local copies, waits for them, and re-layouts: 41.4 us -> none  [the longest x2 31.2 us: resnet_local(): conv_rows(second_act, res_conv_w[res_index, 1]) + res_conv_b[res_index, 1]]
    mul x14 -> x0, local copies, waits for them, and re-layouts: 33.6 us -> none  [the longest x2 30.9 us: group_norm(): grouped * grouped]
where the time goes in v2:
time: 988 us; the launch traced here: 981 us
  Pallas kernels  843 us (85%)
  blocking collectives  62 us (6%)
  waiting for transfers between devices  40.1 us (4%)
  matrix products  15.5 us (2%)
  local copies, waits for them, and re-layouts  15.4 us (2%)
    pallas_call x4, Pallas kernels, conv_call(): pl.pallas_call(functools.partial(conv_kernel, lat_n=lat_n, slot=slot, eps...  328 us
    pallas_call x2, Pallas kernels, ff_call(): pl.pallas_call(functools.partial(ff_kernel, steps=steps, chunk=chunk, lay...  185 us
    pallas_call x2, Pallas kernels, mix_call(): pl.pallas_call(functools.partial(mix_kernel, lat_n=lat_n, layer=layer, ke...  155 us
    pallas_call x2, Pallas kernels, attn_call(): pl.pallas_call(functools.partial(attn_kernel, q_rows=256), grid=(lat_n,),...  62.9 us
    all_to_all x1, blocking collectives, device_block(): lax.all_to_all(last.reshape(own_n, band_n * sp_size, width_n, chan_n), 's...  62 us
    pallas_call x1, Pallas kernels, enter_call(): pl.pallas_call(functools.partial(enter_kernel, lat_n=lat_n, layer=layer),...  52.7 us
    all_to_all x1, waiting for transfers between devices, device_block(): lax.all_to_all(latents, 'sp', 0, 1, tiled=True)  40.1 us
    pallas_call x1, Pallas kernels, heads_call(): pl.pallas_call(functools.partial(heads_kernel, lat_n=lat_n, layer=layer),...  29.5 us
  transfers between devices with their start and end apart: 1, of which 1 were waited for; matrix products, arithmetic and copies ran while one was open for 2% of the time, Pallas kernels for 0%

profile of v2, /device:TPU:0, one launch (start us, length us, event | category | flops | bytes accessed | tf_op | source)
XLA Modules:
  0.0 981.4 jit_solution(4501489028962841373)
XLA Ops:
  0.0 5.2 all-to-all-start
  5.3 2.6 fusion.7
  8.5 2.5 constant_dynamic-slice_fusion
  11.0 0.7 copy.44
  12.9 12.3 %fusion.kc_ref.vc_ref = bf16[2,2,4,80,1280]{4,3,2,1,0:T(8,128)(2,1)} fusion(bf16[2,2,1280,2048,1]{3,2,4,1,0:T(8,128)(2,1)} %bitcast.53, bf16[4,77,2048]{2,1,0:T(8,128)(2,1)S(1)} %copy.44), kind=kOutput, calls=%fused_computation.1 | convolution fusion | flops 6712524800 | bytes 25509888 | tf_op jit(solution)/shard_map/btc,ljdc->ljbtd/dot_general | solution.py:702
  25.2 40.1 %all-to-all-done = bf16[16,2,64,1280]{3,2,1,0:T(8,128)(2,1)} async-done(((bf16[16,2,64,1280]{3,2,1,0:T(8,128)(2,1)}), bf16[16,2,64,1280]{3,2,1,0:T(8,128)(2,1)}, u32[]{:S(2)}, u32[]{:S(2)}) %all-to-all-start) | async-done | bytes 5242912 | tf_op jit(solution)/shard_map/all_to_all | solution.py:689
  65.3 5.4 copy.36
  70.8 11.4 %prep.1.refs_0_ = bf16[4,512,3840]{2,1,0:T(8,128)(2,1)} custom-call(bf16[4,512,1280]{2,1,0:T(8,128)(2,1)} %bitcast.50, f32[2,2,2,1280]{3,2,1,0:T(2,128)} %refs_4_.3, bf16[1280,128]{1,0:T(8,128)(2,1)} %constant.19.clone.tog_ref.refs_5_, bf16[128,1280]{1,0:T(8,128)(2,1)} %constant.20.clone.toc_ref.refs_6_), custom_call_target="tpu_custom_call" | custom-call | tf_op jit(solution)/shard_map/prep/pallas_call | solution.py:113
  82.2 101.8 %conv.4.refs_0_ = bf16[4,512,3840]{2,1,0:T(8,128)(2,1)} custom-call(bf16[4,512,3840]{2,1,0:T(8,128)(2,1)} %prep.1.refs_0_, bf16[4,11520,1280]{2,1,0:T(8,128)(2,1)} %bitcast.3.refs_1_, f32[2,2,1280]{2,1,0:T(2,128)} %refs_2_.7, f32[4,1,1280]{2,1,0:T(1,128)} %broadcast_in_dim.9.refs_3_, f32[2,2,2,1280]{3,2,1,0:T(2,128)} %refs_4_.3, ...), custom_call_target="tpu_custom_call" | custom-call | flops 60397977600 | bytes 29491200 | tf_op jit(solution)/shard_map/conv/pallas_call | solution.py:226
  184.0 71.6 %conv.5 = (bf16[4,512,1280]{2,1,0:T(8,128)(2,1)}, bf16[4,512,1280]{2,1,0:T(8,128)(2,1)}) custom-call(bf16[4,512,3840]{2,1,0:T(8,128)(2,1)} %conv.4.refs_0_, bf16[4,11520,1280]{2,1,0:T(8,128)(2,1)} %bitcast.3.refs_1_, f32[2,2,1280]{2,1,0:T(2,128)} %refs_2_.7, bf16[4,512,1280]{2,1,0:T(8,128)(2,1)} %bitcast.51, f32[1,2,1280]{2,1,0:T(2,128)} %bitcast.60, ...), custom_call_target="tpu_custom_call" | custom-call | flops 60397977600 | bytes 29491200 | tf_op jit(solution)/shard_map/conv/pallas_call | solution.py:226
  255.6 52.7 %enter.1 = (bf16[4,512,1280]{2,1,0:T(8,128)(2,1)}, bf16[4,512,3840]{2,1,0:T(8,128)(2,1)}) custom-call(bf16[4,512,1280]{2,1,0:T(8,128)(2,1)} %get-tuple-element.15.n_ref, bf16[2,1280,1280]{2,1,0:T(8,128)(2,1)} %pw_hbm.3, f32[2,1280]{1,0:T(2,128)} %pb_ref.3, f32[2,3,2,1280]{3,2,1,0:T(2,128)} %ln_ref.7, bf16[2,3,1280,1280]{3,2,1,0:T(8,128)(2,1)} %bitcast.54), custom_call_target="tpu_custom_call" | custom-call | flops 26843545600 | bytes 13107200 | tf_op jit(solution)/shard_map/enter/pallas_call | solution.py:322
  308.4 31.4 %attn.2.o_ref = bf16[4,512,1280]{2,1,0:T(8,128)(2,1)} custom-call(bf16[4,512,3840]{2,1,0:T(8,128)(2,1)} %get-tuple-element.16.q_ref.k_ref.v_ref, bf16[4,512,3840]{2,1,0:T(8,128)(2,1)} %get-tuple-element.16.q_ref.k_ref.v_ref, bf16[4,512,3840]{2,1,0:T(8,128)(2,1)} %get-tuple-element.16.q_ref.k_ref.v_ref), custom_call_target="tpu_custom_call" | custom-call | flops 21474836480 | bytes 20971520 | tf_op jit(solution)/shard_map/attn/pallas_call | solution.py:421
  339.8 77.3 %mix.2 = (bf16[4,512,1280]{2,1,0:T(8,128)(2,1)}, bf16[4,512,1280]{2,1,0:T(8,128)(2,1)}) custom-call(bf16[4,512,1280]{2,1,0:T(8,128)(2,1)} %attn.2.o_ref, bf16[4,512,1280]{2,1,0:T(8,128)(2,1)} %get-tuple-element.17.u_ref, bf16[2,2,4,80,1280]{4,3,2,1,0:T(8,128)(2,1)} %fusion.kc_ref.vc_ref, bf16[2,2,4,80,1280]{4,3,2,1,0:T(8,128)(2,1)} %fusion.kc_ref.vc_ref, ...), custom_call_target="tpu_custom_call" | custom-call | flops 20132659200 | bytes 9830400 | tf_op jit(solution)/shard_map/mix/pallas_call | solution.py:521
  417.1 92.3 %ff.2 = bf16[2048,1280]{1,0:T(8,128)(2,1)} custom-call(bf16[2048,1280]{1,0:T(8,128)(2,1)} %bitcast.67, bf16[2048,1280]{1,0:T(8,128)(2,1)} %bitcast.66, bf16[2,1280,10240]{2,1,0:T(8,128)(2,1)} %wb_ref.3, bf16[2,1280,10240]{2,1,0:T(8,128)(2,1)} %wb_ref.3, f32[2,10240]{1,0:T(2,128)} %bb_ref.3, f32[2,10240]{1,0:T(2,128)} %bb_ref.3, ...), custom_call_target="tpu_custom_call" | custom-call | flops 80530636800 | bytes 39321600 | tf_op jit(solution)/shard_map/ff/pallas_call | solution.py:611
  509.5 29.5 %heads.1.q_ref.k_ref.v_ref = bf16[4,512,3840]{2,1,0:T(8,128)(2,1)} custom-call(bf16[4,512,1280]{2,1,0:T(8,128)(2,1)} %bitcast.61, f32[2,3,2,1280]{3,2,1,0:T(2,128)} %ln_ref.7, bf16[2,3,1280,1280]{3,2,1,0:T(8,128)(2,1)} %bitcast.55), custom_call_target="tpu_custom_call" | custom-call | flops 20132659200 | bytes 9830400 | tf_op jit(solution)/shard_map/heads/pallas_call | solution.py:372
  539.0 31.4 %attn.3.o_ref = bf16[4,512,1280]{2,1,0:T(8,128)(2,1)} custom-call(bf16[4,512,3840]{2,1,0:T(8,128)(2,1)} %heads.1.q_ref.k_ref.v_ref, bf16[4,512,3840]{2,1,0:T(8,128)(2,1)} %heads.1.q_ref.k_ref.v_ref, bf16[4,512,3840]{2,1,0:T(8,128)(2,1)} %heads.1.q_ref.k_ref.v_ref), custom_call_target="tpu_custom_call" | custom-call | flops 21474836480 | bytes 20971520 | tf_op jit(solution)/shard_map/attn/pallas_call | solution.py:421
  570.5 77.3 %mix.3 = (bf16[4,512,1280]{2,1,0:T(8,128)(2,1)}, bf16[4,512,1280]{2,1,0:T(8,128)(2,1)}) custom-call(bf16[4,512,1280]{2,1,0:T(8,128)(2,1)} %attn.3.o_ref, bf16[4,512,1280]{2,1,0:T(8,128)(2,1)} %bitcast.62, bf16[2,2,4,80,1280]{4,3,2,1,0:T(8,128)(2,1)} %fusion.kc_ref.vc_ref, bf16[2,2,4,80,1280]{4,3,2,1,0:T(8,128)(2,1)} %fusion.kc_ref.vc_ref, ...), custom_call_target="tpu_custom_call" | custom-call | flops 20132659200 | bytes 9830400 | tf_op jit(solution)/shard_map/mix/pallas_call | solution.py:521
  647.7 92.3 %ff.3 = bf16[2048,1280]{1,0:T(8,128)(2,1)} custom-call(bf16[2048,1280]{1,0:T(8,128)(2,1)} %bitcast.65, bf16[2048,1280]{1,0:T(8,128)(2,1)} %bitcast.64, bf16[2,1280,10240]{2,1,0:T(8,128)(2,1)} %wb_ref.3, bf16[2,1280,10240]{2,1,0:T(8,128)(2,1)} %wb_ref.3, f32[2,10240]{1,0:T(2,128)} %bb_ref.3, f32[2,10240]{1,0:T(2,128)} %bb_ref.3, ...), custom_call_target="tpu_custom_call" | custom-call | flops 80530636800 | bytes 39321600 | tf_op jit(solution)/shard_map/ff/pallas_call | solution.py:611
  740.0 19.3 %exit.1 = (bf16[4,512,1280]{2,1,0:T(8,128)(2,1)}, bf16[4,512,3840]{2,1,0:T(8,128)(2,1)}) custom-call(bf16[4,512,1280]{2,1,0:T(8,128)(2,1)} %bitcast.63, bf16[4,512,1280]{2,1,0:T(8,128)(2,1)} %get-tuple-element.22.h_ref, bf16[2,1280,1280]{2,1,0:T(8,128)(2,1)} %pw_hbm.3, f32[2,1280]{1,0:T(2,128)} %pb_ref.3, f32[2,2,2,1280]{3,2,1,0:T(2,128)} %refs_4_.3, ...), custom_call_target="tpu_custom_call" | custom-call | flops 6710886400 | bytes 3276800 | tf_op jit(solution)/shard_map/exit/pallas_call | solution.py:671
  759.3 86.0 %conv.6.refs_0_ = bf16[4,512,3840]{2,1,0:T(8,128)(2,1)} custom-call(bf16[4,512,3840]{2,1,0:T(8,128)(2,1)} %get-tuple-element.23.refs_0_, bf16[4,11520,1280]{2,1,0:T(8,128)(2,1)} %bitcast.3.refs_1_, f32[2,2,1280]{2,1,0:T(2,128)} %refs_2_.7, f32[4,1,1280]{2,1,0:T(1,128)} %broadcast_in_dim.11.refs_3_, f32[2,2,2,1280]{3,2,1,0:T(2,128)} %refs_4_.3, ...), custom_call_target="tpu_custom_call" | custom-call | flops 60397977600 | bytes 29491200 | tf_op jit(solution)/shard_map/conv/pallas_call | solution.py:226
  845.3 68.4 %conv.7 = bf16[4,512,1280]{2,1,0:T(8,128)(2,1)} custom-call(bf16[4,512,3840]{2,1,0:T(8,128)(2,1)} %conv.6.refs_0_, bf16[4,11520,1280]{2,1,0:T(8,128)(2,1)} %bitcast.3.refs_1_, f32[2,2,1280]{2,1,0:T(2,128)} %refs_2_.7, bf16[4,512,1280]{2,1,0:T(8,128)(2,1)} %get-tuple-element.24.refs_3_), custom_call_target="tpu_custom_call" | custom-call | flops 60397977600 | bytes 29491200 | tf_op jit(solution)/shard_map/conv/pallas_call | solution.py:226
  913.7 2.8 copy.39
  916.6 62.0 %all_to_all.33 = bf16[4,8,64,1280]{3,2,0,1:T(8,128)(2,1)S(1)} all-to-all(bf16[4,8,64,1280]{3,2,0,1:T(8,128)(2,1)S(1)} %copy.39), channel_id=1, replica_groups=mesh['dp'=2,'sp'=4] {'sp'}, dimensions={1} | all-to-all | bytes 10485760 | tf_op jit(solution)/shard_map/all_to_all | solution.py:721
  978.5 2.7 copy.40
  (10 shorter events, 1.8 us)
Async XLA Ops:
  0.0 5.2 copy-start
  0.0 5.3 copy-start.2
  0.0 65.3 %all-to-all-start = ((bf16[16,2,64,1280]{3,2,1,0:T(8,128)(2,1)}), bf16[16,2,64,1280]{3,2,1,0:T(8,128)(2,1)}, u32[]{:S(2)}, u32[]{:S(2)}) async-start(bf16[16,2,64,1280]{3,2,1,0:T(8,128)(2,1)} %param.31), calls=%async_computation | async-start | bytes 10485760 | tf_op jit(solution)/shard_map/all_to_all | solution.py:689
  5.2 6.5 copy-start.1
